TPU v7x, 128 devices: a whole 4x4x4 slice. The times are simulated.
128 devices in a mesh: tau: 8 (over x, core), tile: 16 (over z, y).
Axes of the slice: x: 4, y: 4, z: 4, core: 2. Of those that a mesh axis runs over, the one named last changes fastest.
Arguments:
- occupied: bfloat16 [8, 2048, 128, 128], P('tau', 'tile'), may hold values from -6 to 6
- virtual: bfloat16 [8, 2048, 128, 128], P('tau', 'tile'), may hold values from -0.125 to 0.125
- cos_weights: float32 [4, 8], replicated, may hold values from -1 to 1
- pair_occ: int32 [3072, 16], P('tile'), may hold values from 0 to 127
- pair_virt: int32 [3072, 16], P('tile'), may hold values from 0 to 127
- partial_target_tile: int32 [3072], P('tile'), may hold values from 0 to 511, as said below
Outputs:
- spectrum: float32 [4, 512, 128, 128], P(None, 'tile', 'tau')
Inputs may be any that keep to these rules, and one draw needn't show every extreme that they name: `partial_target_tile`: within each aligned block of 192 entries, no owner (values d * 32 to (d + 1) * 32 - 1 for owner d) is named more than 24 times; one owner is named exactly 24 times in every block.
All inputs are finite; a program needn't handle non-finite values.
Results may differ from a plain program's by a relative error of at most 0.0003.
Values sent between devices are 32-bit elements; how exact they have to be, the bound alone decides.
No kernel may reach another device: no remote copies, remote signals or barrier semaphores. Data moves between devices by JAX's collectives and lax.ppermute only.
A program may use at most 192 MiB of HBM per device.

v0:
```python
import jax
import jax.numpy as jnp
from jax import lax
from jax.experimental import pallas as pl
from jax.experimental.pallas import tpu as pltpu
from jax.sharding import PartitionSpec as P


TILE = 128
SUB = 8
CHI_DEV = 32
STRIP = 16
TILE_FIRST = (48, 56)
TAU_FIRST = 88
GROUP = 7


def shifts(ntau):
    return [(s, h) for s in range(ntau // 2) for h in range(2)]


def partner(me, shift, ntau, back=False):
    s, h = shift
    chips = ntau // 2
    chip = (me // 2 + (chips - s if back else s)) % chips
    core = (me % 2 + h) % 2
    return 2 * chip + core


def product_of(occ_index, virt_index, occupied, virtual, p, terms, offsets):
    base = p * terms
    slots = [occ_index[base + j] for j in range(terms)]
    strips = [jnp.concatenate([occupied[i, pl.ds(at, STRIP), :] for i in slots], axis=1) for at in offsets]
    left = jnp.concatenate(strips, axis=0)
    right = jnp.concatenate([virtual[virt_index[base + j]] for j in range(terms)], axis=0)
    return jnp.dot(left, right, preferred_element_type=jnp.float32)


def load(pairs, arrived):
    copies = [pltpu.make_async_copy(a, b, arrived.at[i]) for i, (a, b) in enumerate(pairs)]
    for copy in copies:
        copy.start()
    for copy in copies:
        copy.wait()


def strip_offsets(ntau):
    me = lax.axis_index("tau")
    return [pl.multiple_of(partner(me, shift, ntau) * STRIP, STRIP) for shift in shifts(ntau)]


def tile_first_kernel(
    occ_index, virt_index, occ_far, virt_far, *refs, terms, group, start, count, strips, ntau
):
    *given, out, occupied, virtual, arrived = refs
    load([(occ_far, occupied), (virt_far, virtual)], arrived)
    slots = out.shape[1]
    flat = out.reshape(strips * slots * SUB, TILE)
    offsets = strip_offsets(ntau)

    def step(g, carry):
        for q in range(group):
            p = jnp.minimum(g * group + q, count - 1)
            product = product_of(occ_index, virt_index, occupied, virtual, start + p, terms, offsets)
            for v in range(TILE // SUB):
                i, h = divmod(v, 2)
                at = (h * SUB * slots + g * group + q) * SUB + i
                flat[pl.ds(at, SUB, stride=slots * SUB), :] = product[v * SUB : (v + 1) * SUB]
        return carry

    lax.fori_loop(0, slots // group, step, 0)
    for target in given:
        for b in range(strips):
            out[b, slots - 1] = target[...]


def tile_first_products(occ_index, virt_index, occupied, virtual, targets, start, count, terms, strips, ntau):
    far = pl.BlockSpec(memory_space=pltpu.HBM)
    store = pltpu.VMEM(occupied.shape, occupied.dtype)
    slots = count + len(targets)

    def kernel(*refs):
        tile_first_kernel(*refs, terms=terms, group=GROUP, start=start, count=count, strips=strips, ntau=ntau)

    return pl.pallas_call(
        kernel,
        out_shape=jax.ShapeDtypeStruct((strips, slots, SUB, TILE), jnp.float32),
        grid_spec=pltpu.PrefetchScalarGridSpec(
            num_scalar_prefetch=2,
            grid=(1,),
            in_specs=[far, far] + [pl.BlockSpec((SUB, TILE), lambda g, *_: (0, 0))] * len(targets),
            out_specs=pl.BlockSpec((strips, slots, SUB, TILE), lambda g, *_: (0, 0, 0, 0)),
            scratch_shapes=[store, store, pltpu.SemaphoreType.DMA((2,))],
        ),
        compiler_params=pltpu.CompilerParams(vmem_limit_bytes=60 * 2**20),
        name="tile_first_products",
    )(occ_index, virt_index, occupied, virtual, *targets)


def tau_first_kernel(occ_index, virt_index, occ_far, virt_far, *refs, terms, start, ntau):
    *outs, occupied, virtual, arrived = refs
    load([(occ_far, occupied), (virt_far, virtual)], arrived)
    offsets = strip_offsets(ntau)
    count = outs[0].shape[1]
    flats = [out.reshape(STRIP * count, TILE) for out in outs]

    def step(g, carry):
        for q in range(SUB):
            p = g * SUB + q
            product = product_of(occ_index, virt_index, occupied, virtual, start + p, terms, offsets)
            for v in range(TILE // SUB):
                i, h = divmod(v, 2)
                flats[i][pl.ds(h * SUB * count + p, SUB, stride=count), :] = product[v * SUB : (v + 1) * SUB]
        return carry

    lax.fori_loop(0, count // SUB, step, 0)


def tau_first_products(occ_index, virt_index, occupied, virtual, start, count, terms, ntau):
    far = pl.BlockSpec(memory_space=pltpu.HBM)
    store = pltpu.VMEM(occupied.shape, occupied.dtype)

    def kernel(*refs):
        tau_first_kernel(*refs, terms=terms, start=start, ntau=ntau)

    return pl.pallas_call(
        kernel,
        out_shape=[jax.ShapeDtypeStruct((STRIP, count, TILE), jnp.float32)] * ntau,
        grid_spec=pltpu.PrefetchScalarGridSpec(
            num_scalar_prefetch=2,
            grid=(1,),
            in_specs=[far, far],
            out_specs=[pl.BlockSpec((STRIP, count, TILE), lambda g, *_: (0, 0, 0))] * ntau,
            scratch_shapes=[store, store, pltpu.SemaphoreType.DMA((2,))],
        ),
        compiler_params=pltpu.CompilerParams(vmem_limit_bytes=60 * 2**20),
        name="tau_first_products",
    )(occ_index, virt_index, occupied, virtual)


def weigh_kernel(weights, *refs, ntau, nfreq):
    *strips, out = refs
    me = lax.axis_index("tau")
    times = [partner(me, shift, ntau, back=True) for shift in shifts(ntau)]
    scale = [[weights[k * ntau + t] for t in times] for k in range(nfreq)]

    def step(row, carry):
        for at in range(0, out.shape[2], SUB):
            values = [strip[row, at : at + SUB, :] for strip in strips]
            for k in range(nfreq):
                total = scale[k][0] * values[0]
                for t in range(1, ntau):
                    total = total + scale[k][t] * values[t]
                out[row, k, at : at + SUB, :] = total
        return carry

    lax.fori_loop(0, out.shape[0], step, 0)


def weigh(weights, strips, nfreq):
    ntau = len(strips)
    rows, count, width = strips[0].shape
    per = 4

    def kernel(*refs):
        weigh_kernel(*refs, ntau=ntau, nfreq=nfreq)

    return pl.pallas_call(
        kernel,
        out_shape=jax.ShapeDtypeStruct((rows, nfreq, count, width), jnp.float32),
        grid_spec=pltpu.PrefetchScalarGridSpec(
            num_scalar_prefetch=1,
            grid=(rows // per,),
            in_specs=[pl.BlockSpec((per, count, width), lambda g, *_: (g, 0, 0))] * ntau,
            out_specs=pl.BlockSpec((per, nfreq, count, width), lambda g, *_: (g, 0, 0, 0)),
        ),
        compiler_params=pltpu.CompilerParams(vmem_limit_bytes=60 * 2**20),
        name="weigh",
    )(weights, *strips)


BLOCKS = 4


def add_tile_first_kernel(target, *refs, spans, stride):
    n = len(spans)
    pieces, outs, sums = refs[:n], refs[n:-BLOCKS], refs[-BLOCKS:]
    step = pl.program_id(0)

    @pl.when(step == 0)
    def _():
        for acc in sums:
            acc[...] = jnp.zeros_like(acc)

    for (start, count), rows in zip(spans, pieces):

        def add(g, carry, start=start, rows=rows):
            for q in range(SUB):
                p = g * SUB + q
                for block, acc in enumerate(sums):
                    acc[target[(step * BLOCKS + block) * stride + start + p]] += rows[block, p]
            return carry

        lax.fori_loop(0, count // SUB, add, 0)

    @pl.when(step == pl.num_programs(0) - 1)
    def _():
        def turn(g, carry):
            at = pl.multiple_of(g * SUB, SUB)
            total = sum([acc[pl.ds(at, SUB)] for acc in sums[1:]], sums[0][pl.ds(at, SUB)])
            total = jnp.swapaxes(total, 0, 1)
            for i, out in enumerate(outs):
                out[pl.ds(at, SUB), :] = total[i]
            return carry

        lax.fori_loop(0, sums[0].shape[0] // SUB, turn, 0)


def add_tile_first(target, pieces, spans, stride):
    blocks, _, ntau, width = pieces[0].shape
    tiles = blocks * CHI_DEV

    def kernel(*refs):
        add_tile_first_kernel(*refs, spans=spans, stride=stride)

    return pl.pallas_call(
        kernel,
        out_shape=[jax.ShapeDtypeStruct((tiles, width), jnp.float32)] * ntau,
        grid_spec=pltpu.PrefetchScalarGridSpec(
            num_scalar_prefetch=1,
            grid=(blocks // BLOCKS,),
            in_specs=[pl.BlockSpec((BLOCKS, *p.shape[1:]), lambda b, *_: (b, 0, 0, 0)) for p in pieces],
            out_specs=[pl.BlockSpec((tiles, width), lambda b, *_: (0, 0))] * ntau,
            scratch_shapes=[pltpu.VMEM((tiles, ntau, width), jnp.float32)] * BLOCKS,
        ),
        compiler_params=pltpu.CompilerParams(vmem_limit_bytes=60 * 2**20),
        name="add_tile_first",
    )(target, *pieces)


def finish_kernel(target, weights, *refs, starts, stride, ntau, nfreq):
    n = len(starts)
    pieces, times, (out, even, odd) = refs[:n], refs[n : n + ntau], refs[n + ntau :]
    pair = pl.program_id(0)
    me = lax.axis_index("tau")
    origins = [partner(me, shift, ntau, back=True) for shift in shifts(ntau)]
    lower = lax.broadcasted_iota(jnp.int32, (SUB, TILE), 0) < nfreq

    @pl.when(pair == 0)
    def _():
        even[...] = jnp.zeros_like(even)
        odd[...] = jnp.zeros_like(odd)

    for start, piece in zip(starts, pieces):

        def add(g, carry, start=start, piece=piece):
            at = pl.multiple_of(g * SUB, SUB)
            both = jnp.concatenate([piece[0, :, pl.ds(at, SUB), :], piece[1, :, pl.ds(at, SUB), :]], axis=0)
            both = jnp.swapaxes(both, 0, 1)
            base = 2 * pair * stride + start + at
            for q in range(SUB):
                even[target[base + q]] += jnp.where(lower, both[q], 0.0)
                odd[target[base + stride + q]] += jnp.where(lower, 0.0, both[q])
            return carry

        lax.fori_loop(0, piece.shape[2] // SUB, add, 0)

    @pl.when(pair == pl.num_programs(0) - 1)
    def _():
        def step(g, carry):
            at = pl.multiple_of(g * SUB, SUB)
            total = jnp.swapaxes(even[pl.ds(at, SUB)] + odd[pl.ds(at, SUB)], 0, 1)
            values = [part[pl.ds(at, SUB), :] for part in times]
            owner = g // (CHI_DEV // SUB)
            place = pl.multiple_of((g % (CHI_DEV // SUB)) * SUB, SUB)
            for k in range(nfreq):
                value = total[k] + total[k + nfreq]
                for t, part in zip(origins, values):
                    value = value + weights[k * ntau + t] * part
                out[owner, k, pl.ds(place, SUB), :] = value
            return carry

        lax.fori_loop(0, even.shape[0] // SUB, step, 0)


def finish(target, weights, pieces, starts, times, stride, nfreq):
    ntau = len(times)
    tiles, width = times[0].shape
    blocks = tiles // CHI_DEV
    shape = (blocks, nfreq, CHI_DEV, width)

    def kernel(*refs):
        finish_kernel(*refs, starts=starts, stride=stride, ntau=ntau, nfreq=nfreq)

    return pl.pallas_call(
        kernel,
        out_shape=jax.ShapeDtypeStruct(shape, jnp.float32),
        grid_spec=pltpu.PrefetchScalarGridSpec(
            num_scalar_prefetch=2,
            grid=(blocks // 2,),
            in_specs=[pl.BlockSpec((2, nfreq, p.shape[2], width), lambda b, *_: (b, 0, 0, 0)) for p in pieces]
            + [pl.BlockSpec((tiles, width), lambda b, *_: (0, 0))] * ntau,
            out_specs=pl.BlockSpec(shape, lambda b, *_: (0, 0, 0, 0)),
            scratch_shapes=[pltpu.VMEM((tiles, SUB, width), jnp.float32)] * 2,
        ),
        compiler_params=pltpu.CompilerParams(vmem_limit_bytes=50 * 2**20),
        name="finish",
    )(target, weights, *pieces, *times)


def over_tau(strips):
    ntau = len(strips)
    return [strips[0]] + [
        lax.ppermute(strip, "tau", [(i, partner(i, shift, ntau)) for i in range(ntau)])
        for strip, shift in zip(strips[1:], shifts(ntau)[1:])
    ]


def body(occupied, virtual, cos_weights, pair_occ, pair_virt, partial_target_tile):
    ntau = lax.axis_size("tau")
    blocks = lax.axis_size("tile")
    part, terms = pair_occ.shape
    nfreq = cos_weights.shape[0]
    weights = cos_weights.reshape(-1)
    occ_index = pair_occ.reshape(-1)
    virt_index = pair_virt.reshape(-1)
    slot = jnp.pad(partial_target_tile.astype(jnp.float32), (0, SUB * TILE - part)).reshape(SUB, TILE)
    stores = occupied[0], virtual[0]
    first, second = TILE_FIRST
    spans = [(0, first), (first + TAU_FIRST, second)]

    value = tile_first_products(occ_index, virt_index, *stores, [slot], *spans[0], terms, blocks, ntau)
    occ_index, value = lax.optimization_barrier((occ_index, value))
    rows = lax.all_to_all(value, "tile", 0, 0, tiled=True)
    strips = list(tau_first_products(occ_index, virt_index, *stores, first, TAU_FIRST, terms, ntau))
    occ_index, strips[0] = lax.optimization_barrier((occ_index, strips[0]))
    strips = over_tau(strips)
    value = tile_first_products(occ_index, virt_index, *stores, [], *spans[1], terms, blocks, ntau)
    value, rows, weights = lax.optimization_barrier((value, rows, weights))
    more = lax.all_to_all(value, "tile", 0, 0, tiled=True)
    weighted = weigh(weights, strips, nfreq)
    weighted, more = lax.optimization_barrier((weighted, more))
    piece = lax.all_to_all(weighted, "tile", 0, 0, tiled=True)

    lines = -(-part // TILE)
    target = rows[:, first, :lines, :].astype(jnp.int32).reshape(-1)
    stride = lines * TILE
    times = over_tau(add_tile_first(target, [rows, more], spans, stride))
    spectrum = finish(target, weights, [piece], [first], times, stride, nfreq)
    owned = lax.all_to_all(spectrum, "tile", 0, 0, tiled=True)
    return jnp.transpose(owned, (1, 2, 0, 3))


def solution(mesh):
    in_specs = (
        P("tau", "tile", None, None),
        P("tau", "tile", None, None),
        P(),
        P("tile", None),
        P("tile", None),
        P("tile"),
    )
    out_specs = P(None, "tile", "tau", None)

    return jax.shard_map(body, mesh=mesh, in_specs=in_specs, out_specs=out_specs, check_vma=False)
```

profile of v0, /device:TPU:0, one launch (start us, length us, event | category | flops | bytes accessed | tf_op | source)
XLA Modules:
  0.0 240.5 jit_solution(4090772921379993955)
XLA Ops:
  0.0 0.7 convert_element_type.12
  0.7 0.6 pad_bitcast_fusion.refs_4_
  1.3 0.8 copy.8
  2.1 0.7 reshape.15.refs_0_
  2.8 0.8 copy.9
  3.6 0.7 reshape.16.refs_1_
  4.3 15.4 %tile_first_products.2 = f32[16,49,8,128]{3,2,1,0:T(8,128)} custom-call(s32[3072]{0:T(1024)} %reshape.15.refs_0_, s32[3072]{0:T(1024)} %reshape.16.refs_1_, bf16[128,128,128]{2,1,0:T(8,128)(2,1)} %bitcast.8, bf16[128,128,128]{2,1,0:T(8,128)(2,1)} %bitcast.11, f32[8,128]{1,0:T(8,128)} %pad_bitcast_fusion.refs_4_), custom_call_target="tpu_custom_call" | custom-call | tf_op jit(solution)/shard_map/tile_first_products/pallas_call | solution.py:85
  19.7 0.0 copy-start.4
  19.7 8.2 %all-to-all-start = ((f32[16,49,8,128]{3,2,1,0:T(8,128)}), f32[16,49,8,128]{3,2,1,0:T(8,128)S(1)}, u32[]{:S(2)}, u32[]{:S(2)}) async-start(f32[16,49,8,128]{3,2,1,0:T(8,128)} %tile_first_products.2), calls=%async_computation | async-start | bytes 6422528 | tf_op jit(solution)/shard_map/all_to_all | solution.py:334
  27.9 0.6 reshape.18.refs_0_.refs_1_
  28.4 22.1 %tau_first_products.1 = (f32[16,88,128]{2,1,0:T(8,128)}, f32[16,88,128]{2,1,0:T(8,128)}, f32[16,88,128]{2,1,0:T(8,128)}, f32[16,88,128]{2,1,0:T(8,128)}, f32[16,...) custom-call(s32[3072]{0:T(1024)} %reshape.15.refs_0_, ...), custom_call_target="tpu_custom_call" | custom-call | tf_op jit(solution)/shard_map/tau_first_products/pallas_call | solution.py:126
  50.6 18.3 %tile_first_products.3 = f32[16,56,8,128]{3,2,1,0:T(8,128)} custom-call(s32[3072]{0:T(1024)} %reshape.15.refs_0_, s32[3072]{0:T(1024)} %reshape.16.refs_1_, bf16[128,128,128]{2,1,0:T(8,128)(2,1)} %bitcast.10, bf16[128,128,128]{2,1,0:T(8,128)(2,1)} %bitcast.13), custom_call_target="tpu_custom_call" | custom-call | tf_op jit(solution)/shard_map/tile_first_products/pallas_call | solution.py:85
  68.9 7.7 %all-to-all-done.refs_1_ = f32[16,49,8,128]{3,2,1,0:T(8,128)S(1)} async-done(((f32[16,49,8,128]{3,2,1,0:T(8,128)}), f32[16,49,8,128]{3,2,1,0:T(8,128)S(1)}, u32[]{:S(2)}, u32[]{:S(2)}) %all-to-all-start) | async-done | bytes 3211296 | tf_op jit(solution)/shard_map/all_to_all | solution.py:334
  76.6 4.5 %all-to-all-start.1 = ((f32[16,56,8,128]{3,2,1,0:T(8,128)}), f32[16,56,8,128]{3,2,1,0:T(8,128)}, u32[]{:S(2)}, u32[]{:S(2)}) async-start(f32[16,56,8,128]{3,2,1,0:T(8,128)} %tile_first_products.3), calls=%async_computation.1 | async-start | bytes 7340032 | tf_op jit(solution)/shard_map/all_to_all | solution.py:340
  81.1 0.1 collective-permute-start
  81.2 1.2 collective-permute-start.1
  82.5 1.6 collective-permute-start.2
  84.0 1.7 collective-permute-start.3
  85.8 1.5 collective-permute-start.4
  87.3 1.4 collective-permute-start.5
  88.7 13.2 %collective-permute-done.1.refs_3_ = f32[16,88,128]{2,1,0:T(8,128)} collective-permute-done((f32[16,88,128]{2,1,0:T(8,128)}, f32[16,88,128]{2,1,0:T(8,128)}, u32[]{:S(2)}, u32[]{:S(2)}) %collective-permute-start.1) | collective-permute-done | bytes 720928 | tf_op jit(solution)/shard_map/ppermute | solution.py:314
  101.8 0.0 collective-permute-start.6
  101.8 14.4 %collective-permute-done.2.refs_4_ = f32[16,88,128]{2,1,0:T(8,128)} collective-permute-done((f32[16,88,128]{2,1,0:T(8,128)}, f32[16,88,128]{2,1,0:T(8,128)}, u32[]{:S(2)}, u32[]{:S(2)}) %collective-permute-start.2) | collective-permute-done | bytes 720928 | tf_op jit(solution)/shard_map/ppermute | solution.py:314
  116.2 17.2 %collective-permute-done.3.refs_5_ = f32[16,88,128]{2,1,0:T(8,128)} collective-permute-done((f32[16,88,128]{2,1,0:T(8,128)}, f32[16,88,128]{2,1,0:T(8,128)}, u32[]{:S(2)}, u32[]{:S(2)}) %collective-permute-start.3) | collective-permute-done | bytes 720928 | tf_op jit(solution)/shard_map/ppermute | solution.py:314
  133.4 14.4 %collective-permute-done.4.refs_6_ = f32[16,88,128]{2,1,0:T(8,128)} collective-permute-done((f32[16,88,128]{2,1,0:T(8,128)}, f32[16,88,128]{2,1,0:T(8,128)}, u32[]{:S(2)}, u32[]{:S(2)}) %collective-permute-start.4) | collective-permute-done | bytes 720928 | tf_op jit(solution)/shard_map/ppermute | solution.py:314
  147.7 0.0 collective-permute-done.5.refs_7_
  147.7 1.0 collective-permute-done.6.refs_8_
  148.8 6.3 %weigh.1 = f32[16,4,88,128]{3,2,1,0:T(8,128)} custom-call(f32[32]{0:T(128)} %reshape.18.refs_0_.refs_1_, f32[16,88,128]{2,1,0:T(8,128)} %get-tuple-element.36.refs_1_, f32[16,88,128]{2,1,0:T(8,128)} %collective-permute-done.refs_2_, f32[16,88,128]{2,1,0:T(8,128)} %collective-permute-done.1.refs_3_, f32[16,88,128]{2,1,0:T(8,128)} %collective-permute-done.2.refs_4_, ...), custom_call_target="tpu_custom_call" | custom-call | tf_op jit(solution)/shard_map/weigh/pallas_call | solution.py:168
  155.1 7.1 %all-to-all-start.2 = ((f32[16,4,88,128]{3,2,1,0:T(8,128)}), f32[16,4,88,128]{3,2,1,0:T(8,128)}, u32[]{:S(2)}, u32[]{:S(2)}) async-start(f32[16,4,88,128]{3,2,1,0:T(8,128)} %weigh.1), calls=%async_computation.2 | async-start | bytes 5767168 | tf_op jit(solution)/shard_map/all_to_all | solution.py:343
  162.2 0.6 slice_convert_fusion
  162.8 8.9 %add_tile_first.1 = (f32[512,128]{1,0:T(8,128)}, f32[512,128]{1,0:T(8,128)}, f32[512,128]{1,0:T(8,128)}, f32[512,128]{1,0:T(8,128)}, f32[512,128]{1,0:T(8,128)},...) custom-call(s32[4096]{0:T(1024)} %bitcast.6, f32[16,49,8,128]{3,2,1,0:T(8,128)} %copy-done.3, ...), custom_call_target="tpu_custom_call" | custom-call | tf_op jit(solution)/shard_map/add_tile_first/pallas_call | solution.py:226
  171.7 0.2 collective-permute-start.7
  171.8 2.5 %collective-permute-start.8 = (f32[512,128]{1,0:T(8,128)}, f32[512,128]{1,0:T(8,128)S(1)}, u32[]{:S(2)}, u32[]{:S(2)}) collective-permute-start(f32[512,128]{1,0:T(8,128)} %get-tuple-element.49), channel_id=1, source_target_pairs={{0,32},{16,48},{32,64},{48,80},{64,96},{80,112},{96,0},{112,16},{1... | collective-permute-start | bytes 786440 | tf_op jit(solution)/shard_map/ppermute | solution.py:314
  174.4 0.1 collective-permute-start.9
  174.4 2.0 collective-permute-start.10
  176.4 1.0 collective-permute-start.11
  177.5 3.1 %collective-permute-start.12 = (f32[512,128]{1,0:T(8,128)}, f32[512,128]{1,0:T(8,128)S(1)}, u32[]{:S(2)}, u32[]{:S(2)}) collective-permute-start(f32[512,128]{1,0:T(8,128)} %get-tuple-element.53), channel_id=1, source_target_pairs={{0,96},{16,112},{32,0},{48,16},{64,32},{80,48},{96,64},{112,80},{1... | collective-permute-start | bytes 786440 | tf_op jit(solution)/shard_map/ppermute | solution.py:314
  180.6 1.9 collective-permute-done.8.refs_5_
  182.4 0.7 collective-permute-start.13
  183.1 4.2 %collective-permute-done.9.refs_6_ = f32[512,128]{1,0:T(8,128)S(1)} collective-permute-done((f32[512,128]{1,0:T(8,128)}, f32[512,128]{1,0:T(8,128)S(1)}, u32[]{:S(2)}, u32[]{:S(2)}) %collective-permute-start.9) | collective-permute-done | bytes 262176 | tf_op jit(solution)/shard_map/ppermute | solution.py:314
  187.3 7.7 %collective-permute-done.10.refs_7_ = f32[512,128]{1,0:T(8,128)S(1)} collective-permute-done((f32[512,128]{1,0:T(8,128)}, f32[512,128]{1,0:T(8,128)S(1)}, u32[]{:S(2)}, u32[]{:S(2)}) %collective-permute-start.10) | collective-permute-done | bytes 262176 | tf_op jit(solution)/shard_map/ppermute | solution.py:314
  195.0 4.6 %collective-permute-done.11.refs_8_ = f32[512,128]{1,0:T(8,128)S(1)} collective-permute-done((f32[512,128]{1,0:T(8,128)}, f32[512,128]{1,0:T(8,128)S(1)}, u32[]{:S(2)}, u32[]{:S(2)}) %collective-permute-start.11) | collective-permute-done | bytes 262176 | tf_op jit(solution)/shard_map/ppermute | solution.py:314
  199.6 1.6 collective-permute-done.13.refs_10_
  201.2 6.3 %all-to-all-done.2.refs_2_ = f32[16,4,88,128]{3,2,1,0:T(8,128)} async-done(((f32[16,4,88,128]{3,2,1,0:T(8,128)}), f32[16,4,88,128]{3,2,1,0:T(8,128)}, u32[]{:S(2)}, u32[]{:S(2)}) %all-to-all-start.2) | async-done | bytes 2883616 | tf_op jit(solution)/shard_map/all_to_all | solution.py:343
  207.5 0.9 copy-done
  208.5 9.8 %finish.1 = f32[16,4,32,128]{3,2,1,0:T(8,128)S(1)} custom-call(s32[4096]{0:T(1024)S(1)} %bitcast.7, f32[32]{0:T(128)S(1)} %copy-done.2, f32[16,4,88,128]{3,2,1,0:T(8,128)} %all-to-all-done.2.refs_2_, f32[512,128]{1,0:T(8,128)S(1)} %copy-done, f32[512,128]{1,0:T(8,128)S(1)} %collective-permute-done.7.refs_4_, f32[512,128]{1,0:T(8,128)S(1)} %collective-permute-done.8.refs_5_, ...), custom_call_target="tpu_custom_call" | custom-call | tf_op jit(solution)/shard_map/finish/pallas_call | solution.py:295
  218.3 20.6 %all_to_all.20 = f32[16,4,32,128]{3,2,1,0:T(8,128)S(1)} all-to-all(f32[16,4,32,128]{3,2,1,0:T(8,128)S(1)} %finish.1), channel_id=1, replica_groups=mesh['tau'=8,'tile'=16] {'tile'}, dimensions={0} | all-to-all | bytes 2097152 | tf_op jit(solution)/shard_map/all_to_all | solution.py:350
  238.9 1.6 copy.10
  (12 shorter events, 0.0 us)
Async XLA Ops:
  19.7 8.2 %copy-start.4 = (f32[4,8]{1,0:T(4,128)S(1)}, f32[4,8]{1,0:T(4,128)}, u32[]{:S(2)}) copy-start(f32[4,8]{1,0:T(4,128)} %param.8) | copy-start | bytes 388
  19.7 56.9 %all-to-all-start = ((f32[16,49,8,128]{3,2,1,0:T(8,128)}), f32[16,49,8,128]{3,2,1,0:T(8,128)S(1)}, u32[]{:S(2)}, u32[]{:S(2)}) async-start(f32[16,49,8,128]{3,2,1,0:T(8,128)} %tile_first_products.2), calls=%async_computation | async-start | bytes 6422528 | tf_op jit(solution)/shard_map/all_to_all | solution.py:334
  76.6 85.6 %copy-start.3 = (f32[16,49,8,128]{3,2,1,0:T(8,128)}, f32[16,49,8,128]{3,2,1,0:T(8,128)S(1)}, u32[]{:S(2)}) copy-start(f32[16,49,8,128]{3,2,1,0:T(8,128)S(1)} %all-to-all-done.refs_1_) | copy-start | bytes 9633796
  76.6 78.4 %all-to-all-start.1 = ((f32[16,56,8,128]{3,2,1,0:T(8,128)}), f32[16,56,8,128]{3,2,1,0:T(8,128)}, u32[]{:S(2)}, u32[]{:S(2)}) async-start(f32[16,56,8,128]{3,2,1,0:T(8,128)} %tile_first_products.3), calls=%async_computation.1 | async-start | bytes 7340032 | tf_op jit(solution)/shard_map/all_to_all | solution.py:340
  81.1 6.1 %collective-permute-start = (f32[16,88,128]{2,1,0:T(8,128)}, f32[16,88,128]{2,1,0:T(8,128)}, u32[]{:S(2)}, u32[]{:S(2)}) collective-permute-start(f32[16,88,128]{2,1,0:T(8,128)} %get-tuple-element.37), channel_id=1, source_target_pairs={{0,16},{16,0},{32,48},{48,32},{64,80},{80,64},{96,112},{112,96},{1... | collective-permute-start | bytes 2162696 | tf_op jit(solution)/shard_map/ppermute | solution.py:314
  81.2 20.6 %collective-permute-start.1 = (f32[16,88,128]{2,1,0:T(8,128)}, f32[16,88,128]{2,1,0:T(8,128)}, u32[]{:S(2)}, u32[]{:S(2)}) collective-permute-start(f32[16,88,128]{2,1,0:T(8,128)} %get-tuple-element.38), channel_id=1, source_target_pairs={{0,32},{16,48},{32,64},{48,80},{64,96},{80,112},{96,0},{112,16},{1... | collective-permute-start | bytes 2162696 | tf_op jit(solution)/shard_map/ppermute | solution.py:314
  82.5 33.7 %collective-permute-start.2 = (f32[16,88,128]{2,1,0:T(8,128)}, f32[16,88,128]{2,1,0:T(8,128)}, u32[]{:S(2)}, u32[]{:S(2)}) collective-permute-start(f32[16,88,128]{2,1,0:T(8,128)} %get-tuple-element.39), channel_id=1, source_target_pairs={{0,48},{16,32},{32,80},{48,64},{64,112},{80,96},{96,16},{112,0},{1... | collective-permute-start | bytes 2162696 | tf_op jit(solution)/shard_map/ppermute | solution.py:314
  84.0 49.4 %collective-permute-start.3 = (f32[16,88,128]{2,1,0:T(8,128)}, f32[16,88,128]{2,1,0:T(8,128)}, u32[]{:S(2)}, u32[]{:S(2)}) collective-permute-start(f32[16,88,128]{2,1,0:T(8,128)} %get-tuple-element.40), channel_id=1, source_target_pairs={{0,64},{16,80},{32,96},{48,112},{64,0},{80,16},{96,32},{112,48},{1... | collective-permute-start | bytes 2162696 | tf_op jit(solution)/shard_map/ppermute | solution.py:314
  85.8 62.0 %collective-permute-start.4 = (f32[16,88,128]{2,1,0:T(8,128)}, f32[16,88,128]{2,1,0:T(8,128)}, u32[]{:S(2)}, u32[]{:S(2)}) collective-permute-start(f32[16,88,128]{2,1,0:T(8,128)} %get-tuple-element.41), channel_id=1, source_target_pairs={{0,80},{16,64},{32,112},{48,96},{64,16},{80,0},{96,48},{112,32},{1... | collective-permute-start | bytes 2162696 | tf_op jit(solution)/shard_map/ppermute | solution.py:314
  87.3 60.5 %collective-permute-start.5 = (f32[16,88,128]{2,1,0:T(8,128)}, f32[16,88,128]{2,1,0:T(8,128)}, u32[]{:S(2)}, u32[]{:S(2)}) collective-permute-start(f32[16,88,128]{2,1,0:T(8,128)} %get-tuple-element.42), channel_id=1, source_target_pairs={{0,96},{16,112},{32,0},{48,16},{64,32},{80,48},{96,64},{112,80},{1... | collective-permute-start | bytes 2162696 | tf_op jit(solution)/shard_map/ppermute | solution.py:314
  101.8 46.9 %collective-permute-start.6 = (f32[16,88,128]{2,1,0:T(8,128)}, f32[16,88,128]{2,1,0:T(8,128)}, u32[]{:S(2)}, u32[]{:S(2)}) collective-permute-start(f32[16,88,128]{2,1,0:T(8,128)} %get-tuple-element.43), channel_id=1, source_target_pairs={{0,112},{16,96},{32,16},{48,0},{64,48},{80,32},{96,80},{112,64},{1... | collective-permute-start | bytes 2162696 | tf_op jit(solution)/shard_map/ppermute | solution.py:314
  155.1 52.5 %all-to-all-start.2 = ((f32[16,4,88,128]{3,2,1,0:T(8,128)}), f32[16,4,88,128]{3,2,1,0:T(8,128)}, u32[]{:S(2)}, u32[]{:S(2)}) async-start(f32[16,4,88,128]{3,2,1,0:T(8,128)} %weigh.1), calls=%async_computation.2 | async-start | bytes 5767168 | tf_op jit(solution)/shard_map/all_to_all | solution.py:343
  162.8 44.7 %copy-start.1 = (s32[16,1,2,128]{3,2,1,0:T(2,128)S(1)}, s32[16,1,2,128]{3,2,1,0:T(2,128)}, u32[]{:S(2)}) copy-start(s32[16,1,2,128]{3,2,1,0:T(2,128)} %slice_convert_fusion) | copy-start | bytes 49156
  162.8 44.7 %copy-start.2 = (f32[32]{0:T(128)S(1)}, f32[32]{0:T(128)}, u32[]{:S(2)}) copy-start(f32[32]{0:T(128)} %reshape.18.refs_0_.refs_1_) | copy-start | bytes 388
  171.7 5.8 %collective-permute-start.7 = (f32[512,128]{1,0:T(8,128)}, f32[512,128]{1,0:T(8,128)S(1)}, u32[]{:S(2)}, u32[]{:S(2)}) collective-permute-start(f32[512,128]{1,0:T(8,128)} %get-tuple-element.48), channel_id=1, source_target_pairs={{0,16},{16,0},{32,48},{48,32},{64,80},{80,64},{96,112},{112,96},{1... | collective-permute-start | bytes 786440 | tf_op jit(solution)/shard_map/ppermute | solution.py:314
  171.8 10.6 %collective-permute-start.8 = (f32[512,128]{1,0:T(8,128)}, f32[512,128]{1,0:T(8,128)S(1)}, u32[]{:S(2)}, u32[]{:S(2)}) collective-permute-start(f32[512,128]{1,0:T(8,128)} %get-tuple-element.49), channel_id=1, source_target_pairs={{0,32},{16,48},{32,64},{48,80},{64,96},{80,112},{96,0},{112,16},{1... | collective-permute-start | bytes 786440 | tf_op jit(solution)/shard_map/ppermute | solution.py:314
  174.4 12.9 %collective-permute-start.9 = (f32[512,128]{1,0:T(8,128)}, f32[512,128]{1,0:T(8,128)S(1)}, u32[]{:S(2)}, u32[]{:S(2)}) collective-permute-start(f32[512,128]{1,0:T(8,128)} %get-tuple-element.50), channel_id=1, source_target_pairs={{0,48},{16,32},{32,80},{48,64},{64,112},{80,96},{96,16},{112,0},{1... | collective-permute-start | bytes 786440 | tf_op jit(solution)/shard_map/ppermute | solution.py:314
  174.4 20.5 %collective-permute-start.10 = (f32[512,128]{1,0:T(8,128)}, f32[512,128]{1,0:T(8,128)S(1)}, u32[]{:S(2)}, u32[]{:S(2)}) collective-permute-start(f32[512,128]{1,0:T(8,128)} %get-tuple-element.51), channel_id=1, source_target_pairs={{0,64},{16,80},{32,96},{48,112},{64,0},{80,16},{96,32},{112,48},{1... | collective-permute-start | bytes 786440 | tf_op jit(solution)/shard_map/ppermute | solution.py:314
  176.4 23.1 %collective-permute-start.11 = (f32[512,128]{1,0:T(8,128)}, f32[512,128]{1,0:T(8,128)S(1)}, u32[]{:S(2)}, u32[]{:S(2)}) collective-permute-start(f32[512,128]{1,0:T(8,128)} %get-tuple-element.52), channel_id=1, source_target_pairs={{0,80},{16,64},{32,112},{48,96},{64,16},{80,0},{96,48},{112,32},{1... | collective-permute-start | bytes 786440 | tf_op jit(solution)/shard_map/ppermute | solution.py:314
  177.5 22.1 %collective-permute-start.12 = (f32[512,128]{1,0:T(8,128)}, f32[512,128]{1,0:T(8,128)S(1)}, u32[]{:S(2)}, u32[]{:S(2)}) collective-permute-start(f32[512,128]{1,0:T(8,128)} %get-tuple-element.53), channel_id=1, source_target_pairs={{0,96},{16,112},{32,0},{48,16},{64,32},{80,48},{96,64},{112,80},{1... | collective-permute-start | bytes 786440 | tf_op jit(solution)/shard_map/ppermute | solution.py:314
  182.4 18.8 %collective-permute-start.13 = (f32[512,128]{1,0:T(8,128)}, f32[512,128]{1,0:T(8,128)S(1)}, u32[]{:S(2)}, u32[]{:S(2)}) collective-permute-start(f32[512,128]{1,0:T(8,128)} %get-tuple-element.54), channel_id=1, source_target_pairs={{0,112},{16,96},{32,16},{48,0},{64,48},{80,32},{96,80},{112,64},{1... | collective-permute-start | bytes 786440 | tf_op jit(solution)/shard_map/ppermute | solution.py:314
  207.5 1.0 copy-start
where the time goes:
time: 242 us; the launch traced here: 240 us
  waiting for transfers between devices  94.1 us (39%)
  Pallas kernels  80.8 us (33%)
  starting transfers between devices  36.9 us (15%)
  blocking collectives  20.6 us (9%)
  local copies, waits for them, and re-layouts  6.72 us (3%)
    ppermute x14, waiting for transfers between devices, over_tau(): lax.ppermute(strip, 'tau', [(i, partner(i, shift, ntau)) for i in range(n...  80.1 us
    pallas_call x2, Pallas kernels, tile_first_products(): pl.pallas_call(kernel, out_shape=jax.ShapeDtypeStruct((strips, slots, SUB...  33.7 us
    pallas_call x1, Pallas kernels, tau_first_products(): pl.pallas_call(kernel, out_shape=[jax.ShapeDtypeStruct((STRIP, count, TIL...  22.1 us
    all_to_all x1, blocking collectives, body(): owned = lax.all_to_all(spectrum, 'tile', 0, 0, tiled=True)  20.6 us
    ppermute x14, starting transfers between devices, over_tau(): lax.ppermute(strip, 'tau', [(i, partner(i, shift, ntau)) for i in range(n...  17.1 us
    pallas_call x1, Pallas kernels, finish(): pl.pallas_call(kernel, out_shape=jax.ShapeDtypeStruct(shape, jnp.float32)...  9.82 us
    pallas_call x1, Pallas kernels, add_tile_first(): pl.pallas_call(kernel, out_shape=[jax.ShapeDtypeStruct((tiles, width), jn...  8.88 us
    all_to_all x1, starting transfers between devices, body(): rows = lax.all_to_all(value, 'tile', 0, 0, tiled=True)  8.17 us
  transfers between devices with their start and end apart: 17, of which 12 were waited for; matrix products, arithmetic and copies ran while one was open for 0% of the time, Pallas kernels for 23%

commit v1 on v0

v1 whole, which is shorter than its diff:
```python
import jax
import jax.numpy as jnp
from jax import lax
from jax.experimental import pallas as pl
from jax.experimental.pallas import tpu as pltpu
from jax.sharding import PartitionSpec as P


TILE = 128
SUB = 8
CHI_DEV = 32
STRIP = 16
TILE_FIRST = (56, 56)
TAU_FIRST = 80
SIDE = 4


def shifts(ntau):
    return [(s, h) for s in range(ntau // 2) for h in range(2)]


def partner(me, shift, ntau, back=False):
    s, h = shift
    chips = ntau // 2
    chip = (me // 2 + (chips - s if back else s)) % chips
    core = (me % 2 + h) % 2
    return 2 * chip + core


def product_of(occ_index, virt_index, occupied, virtual, p, terms, offsets):
    slots = [occ_index[j, p] for j in range(terms)]
    strips = [jnp.concatenate([occupied[i, pl.ds(at, STRIP), :] for i in slots], axis=1) for at in offsets]
    left = jnp.concatenate(strips, axis=0)
    right = jnp.concatenate([virtual[virt_index[j, p]] for j in range(terms)], axis=0)
    return jnp.dot(left, right, preferred_element_type=jnp.float32)


def load(pairs, arrived):
    copies = [pltpu.make_async_copy(a, b, arrived.at[i]) for i, (a, b) in enumerate(pairs)]
    for copy in copies:
        copy.start()
    for copy in copies:
        copy.wait()


def strip_offsets(ntau):
    me = lax.axis_index("tau")
    return [pl.multiple_of(partner(me, shift, ntau) * STRIP, STRIP) for shift in shifts(ntau)]


def around(me, s, u, z_first, back=False):
    dz, dy = (s, u) if z_first else (u, s)
    z, y = me // SIDE, me % SIDE
    if back:
        return (z + SIDE - dz) % SIDE * SIDE + (y + SIDE - dy) % SIDE
    return (z + dz) % SIDE * SIDE + (y + dy) % SIDE


def tile_first_kernel(occ_index, virt_index, occ_far, virt_far, *refs, terms, start, count, ntau, z_first, given):
    target, outs, (rows, occupied, virtual, arrived, left) = refs[:given], refs[given : given + SIDE], refs[given + SIDE :]
    load([(occ_far, occupied), (virt_far, virtual)], arrived)
    strips, slots = rows.shape[:2]
    flat = rows.reshape(strips * slots * SUB, TILE)
    offsets = strip_offsets(ntau)

    def step(g, carry):
        for q in range(SUB):
            p = g * SUB + q
            product = product_of(occ_index, virt_index, occupied, virtual, start + p, terms, offsets)
            for v in range(TILE // SUB):
                i, h = divmod(v, 2)
                at = (h * SUB * slots + p) * SUB + i
                flat[pl.ds(at, SUB, stride=slots * SUB), :] = product[v * SUB : (v + 1) * SUB]
        return carry

    lax.fori_loop(0, count // SUB, step, 0)
    for ref in target:
        for b in range(strips):
            rows[b, count] = ref[...]
    me = lax.axis_index("tile")
    copies = []
    for s in range(SIDE):
        for u in range(SIDE):
            source = rows.at[around(me, s, u, z_first), pl.ds(0, count + given)]
            copies.append(pltpu.make_async_copy(source, outs[s].at[u], left.at[s * SIDE + u]))
    for copy in copies:
        copy.start()
    for copy in copies:
        copy.wait()


def tile_first_products(occ_index, virt_index, occupied, virtual, targets, start, count, terms, strips, ntau, z_first):
    far = pl.BlockSpec(memory_space=pltpu.HBM)
    store = pltpu.VMEM(occupied.shape, occupied.dtype)
    given = len(targets)

    def kernel(*refs):
        tile_first_kernel(*refs, terms=terms, start=start, count=count, ntau=ntau, z_first=z_first, given=given)

    return pl.pallas_call(
        kernel,
        out_shape=[jax.ShapeDtypeStruct((SIDE, count + given, SUB, TILE), jnp.float32)] * SIDE,
        grid_spec=pltpu.PrefetchScalarGridSpec(
            num_scalar_prefetch=2,
            grid=(1,),
            in_specs=[far, far] + [pl.BlockSpec((SUB, TILE), lambda g, *_: (0, 0))] * given,
            out_specs=[far] * SIDE,
            scratch_shapes=[
                pltpu.VMEM((strips, count + 1, SUB, TILE), jnp.float32),
                store,
                store,
                pltpu.SemaphoreType.DMA((2,)),
                pltpu.SemaphoreType.DMA((strips,)),
            ],
        ),
        compiler_params=pltpu.CompilerParams(vmem_limit_bytes=60 * 2**20),
        name="tile_first_products",
    )(occ_index, virt_index, occupied, virtual, *targets)


def tau_first_kernel(occ_index, virt_index, occ_far, virt_far, *refs, terms, start, ntau):
    *outs, occupied, virtual, arrived = refs
    load([(occ_far, occupied), (virt_far, virtual)], arrived)
    offsets = strip_offsets(ntau)
    count = outs[0].shape[1]
    flats = [out.reshape(STRIP * count, TILE) for out in outs]

    def step(g, carry):
        for q in range(SUB):
            p = g * SUB + q
            product = product_of(occ_index, virt_index, occupied, virtual, start + p, terms, offsets)
            for v in range(TILE // SUB):
                i, h = divmod(v, 2)
                flats[i][pl.ds(h * SUB * count + p, SUB, stride=count), :] = product[v * SUB : (v + 1) * SUB]
        return carry

    lax.fori_loop(0, count // SUB, step, 0)


def tau_first_products(occ_index, virt_index, occupied, virtual, start, count, terms, ntau):
    far = pl.BlockSpec(memory_space=pltpu.HBM)
    store = pltpu.VMEM(occupied.shape, occupied.dtype)

    def kernel(*refs):
        tau_first_kernel(*refs, terms=terms, start=start, ntau=ntau)

    return pl.pallas_call(
        kernel,
        out_shape=[jax.ShapeDtypeStruct((STRIP, count, TILE), jnp.float32)] * ntau,
        grid_spec=pltpu.PrefetchScalarGridSpec(
            num_scalar_prefetch=2,
            grid=(1,),
            in_specs=[far, far],
            out_specs=[pl.BlockSpec((STRIP, count, TILE), lambda g, *_: (0, 0, 0))] * ntau,
            scratch_shapes=[store, store, pltpu.SemaphoreType.DMA((2,))],
        ),
        compiler_params=pltpu.CompilerParams(vmem_limit_bytes=60 * 2**20),
        name="tau_first_products",
    )(occ_index, virt_index, occupied, virtual)


def weigh_kernel(weights, *refs, ntau, nfreq):
    *strips, out = refs
    me = lax.axis_index("tau")
    times = [partner(me, shift, ntau, back=True) for shift in shifts(ntau)]
    scale = [[weights[k * ntau + t] for t in times] for k in range(nfreq)]

    def step(row, carry):
        for at in range(0, out.shape[2], SUB):
            values = [strip[row, at : at + SUB, :] for strip in strips]
            for k in range(nfreq):
                total = scale[k][0] * values[0]
                for t in range(1, ntau):
                    total = total + scale[k][t] * values[t]
                out[row, k, at : at + SUB, :] = total
        return carry

    lax.fori_loop(0, out.shape[0], step, 0)


def weigh(weights, strips, nfreq):
    ntau = len(strips)
    rows, count, width = strips[0].shape
    per = 4

    def kernel(*refs):
        weigh_kernel(*refs, ntau=ntau, nfreq=nfreq)

    return pl.pallas_call(
        kernel,
        out_shape=jax.ShapeDtypeStruct((rows, nfreq, count, width), jnp.float32),
        grid_spec=pltpu.PrefetchScalarGridSpec(
            num_scalar_prefetch=1,
            grid=(rows // per,),
            in_specs=[pl.BlockSpec((per, count, width), lambda g, *_: (g, 0, 0))] * ntau,
            out_specs=pl.BlockSpec((per, nfreq, count, width), lambda g, *_: (g, 0, 0, 0)),
        ),
        compiler_params=pltpu.CompilerParams(vmem_limit_bytes=60 * 2**20),
        name="weigh",
    )(weights, *strips)


def add_tile_first_kernel(target, *refs, spans, stride, ntau):
    sums, outs = refs[-SIDE:], refs[-SIDE - ntau : -SIDE]
    for acc in sums:
        acc[...] = jnp.zeros_like(acc)
    for half, (start, count) in enumerate(spans):
        near, far = refs[half * (2 * SIDE - 1) :][:SIDE], refs[half * (2 * SIDE - 1) + SIDE :][: SIDE - 1]
        for u in range(SIDE):
            rows = [far[u - 1].at[s] if u else near[s].at[0] for s in range(SIDE)]
            places = [(s, u) if half == 0 else (u, s) for s in range(SIDE)]
            bases = [(dz * SIDE + dy) * stride + start for dz, dy in places]

            def add(g, carry, rows=rows, bases=bases):
                for q in range(SUB):
                    p = g * SUB + q
                    for ref, base, acc in zip(rows, bases, sums):
                        acc[target[base + p]] += ref[p]
                return carry

            lax.fori_loop(0, count // SUB, add, 0)

    def turn(g, carry):
        at = pl.multiple_of(g * SUB, SUB)
        total = sum([acc[pl.ds(at, SUB)] for acc in sums[1:]], sums[0][pl.ds(at, SUB)])
        total = jnp.swapaxes(total, 0, 1)
        for i, out in enumerate(outs):
            out[pl.ds(at, SUB), :] = total[i]
        return carry

    lax.fori_loop(0, sums[0].shape[0] // SUB, turn, 0)


def add_tile_first(target, halves, spans, stride, ntau):
    tiles = SIDE * SIDE * CHI_DEV
    operands, specs = [], []
    for near, far in halves:
        operands += [*near, *far]
        specs += [pl.BlockSpec((1, *p.shape[1:]), lambda b, *_: (0, 0, 0, 0)) for p in near]
        specs += [pl.BlockSpec(p.shape, lambda b, *_: (0, 0, 0, 0)) for p in far]

    def kernel(*refs):
        add_tile_first_kernel(*refs, spans=spans, stride=stride, ntau=ntau)

    return pl.pallas_call(
        kernel,
        out_shape=[jax.ShapeDtypeStruct((tiles, TILE), jnp.float32)] * ntau,
        grid_spec=pltpu.PrefetchScalarGridSpec(
            num_scalar_prefetch=1,
            grid=(1,),
            in_specs=specs,
            out_specs=[pl.BlockSpec((tiles, TILE), lambda b, *_: (0, 0))] * ntau,
            scratch_shapes=[pltpu.VMEM((tiles, ntau, TILE), jnp.float32)] * SIDE,
        ),
        compiler_params=pltpu.CompilerParams(vmem_limit_bytes=60 * 2**20),
        name="add_tile_first",
    )(target, *operands)


def finish_kernel(target, weights, piece, *refs, start, stride, ntau, nfreq):
    times, out, sums = refs[:ntau], refs[ntau], refs[ntau + 1 :]
    step = pl.program_id(0)
    here = lax.axis_index("tau")
    origins = [partner(here, shift, ntau, back=True) for shift in shifts(ntau)]
    lower = lax.broadcasted_iota(jnp.int32, (SUB, TILE), 0) < nfreq
    me = lax.axis_index("tile")
    dz = (me // SIDE + SIDE - step) % SIDE
    bases = [(dz * SIDE + (me % SIDE + SIDE - y) % SIDE) * stride + start for y in range(SIDE)]

    @pl.when(step == 0)
    def _():
        for acc in sums:
            acc[...] = jnp.zeros_like(acc)

    def add(g, carry):
        at = pl.multiple_of(g * SUB, SUB)
        blocks = [piece[i, :, pl.ds(at, SUB), :] for i in range(SIDE)]
        pairs = [jnp.swapaxes(jnp.concatenate(blocks[i : i + 2], axis=0), 0, 1) for i in (0, 2)]
        for q in range(SUB):
            for i in range(SIDE):
                both = pairs[i // 2][q]
                mine = jnp.where(lower, 0.0, both) if i % 2 else jnp.where(lower, both, 0.0)
                sums[i][target[bases[i] + at + q]] += mine
        return carry

    lax.fori_loop(0, piece.shape[2] // SUB, add, 0)

    @pl.when(step == pl.num_programs(0) - 1)
    def _():
        def last(g, carry):
            at = pl.multiple_of(g * SUB, SUB)
            total = sum([acc[pl.ds(at, SUB)] for acc in sums[1:]], sums[0][pl.ds(at, SUB)])
            total = jnp.swapaxes(total, 0, 1)
            values = [part[pl.ds(at, SUB), :] for part in times]
            owner = g // (CHI_DEV // SUB)
            place = pl.multiple_of((g % (CHI_DEV // SUB)) * SUB, SUB)
            for k in range(nfreq):
                value = total[k] + total[k + nfreq]
                for t, part in zip(origins, values):
                    value = value + weights[k * ntau + t] * part
                out[owner, k, pl.ds(place, SUB), :] = value
            return carry

        lax.fori_loop(0, sums[0].shape[0] // SUB, last, 0)


def finish(target, weights, piece, start, times, stride, nfreq):
    ntau = len(times)
    tiles, width = times[0].shape
    blocks = tiles // CHI_DEV
    shape = (blocks, nfreq, CHI_DEV, width)

    def kernel(*refs):
        finish_kernel(*refs, start=start, stride=stride, ntau=ntau, nfreq=nfreq)

    return pl.pallas_call(
        kernel,
        out_shape=jax.ShapeDtypeStruct(shape, jnp.float32),
        grid_spec=pltpu.PrefetchScalarGridSpec(
            num_scalar_prefetch=2,
            grid=(blocks // SIDE,),
            in_specs=[pl.BlockSpec((SIDE, nfreq, piece.shape[2], width), lambda b, *_: (b, 0, 0, 0))]
            + [pl.BlockSpec((tiles, width), lambda b, *_: (0, 0))] * ntau,
            out_specs=pl.BlockSpec(shape, lambda b, *_: (0, 0, 0, 0)),
            scratch_shapes=[pltpu.VMEM((tiles, SUB, width), jnp.float32)] * SIDE,
        ),
        compiler_params=pltpu.CompilerParams(vmem_limit_bytes=50 * 2**20),
        name="finish",
    )(target, weights, piece, *times)


def turn_kernel(*refs):
    near, outs, arrived = refs[:SIDE], refs[SIDE:-1], refs[-1]
    copies = []
    for u in range(1, SIDE):
        for s in range(SIDE):
            copies.append(pltpu.make_async_copy(near[s].at[u], outs[u - 1].at[s], arrived.at[(u - 1) * SIDE + s]))
    for copy in copies:
        copy.start()
    for copy in copies:
        copy.wait()


def turn(near):
    anywhere = pl.BlockSpec(memory_space=pltpu.HBM)
    return pl.pallas_call(
        turn_kernel,
        out_shape=[jax.ShapeDtypeStruct(near[0].shape, jnp.float32)] * (SIDE - 1),
        in_specs=[anywhere] * SIDE,
        out_specs=[anywhere] * (SIDE - 1),
        scratch_shapes=[pltpu.SemaphoreType.DMA((SIDE * (SIDE - 1),))],
        compiler_params=pltpu.CompilerParams(vmem_limit_bytes=60 * 2**20),
        name="turn",
    )(*near)


def over_tau(strips):
    ntau = len(strips)
    return [strips[0]] + [
        lax.ppermute(strip, "tau", [(i, partner(i, shift, ntau)) for i in range(ntau)])
        for strip, shift in zip(strips[1:], shifts(ntau)[1:])
    ]


def over_tile(rows, s, u, z_first):
    n = SIDE * SIDE
    return lax.ppermute(rows, "tile", [(i, around(i, s, u, z_first)) for i in range(n)])


def body(occupied, virtual, cos_weights, pair_occ, pair_virt, partial_target_tile):
    ntau = lax.axis_size("tau")
    blocks = lax.axis_size("tile")
    part, terms = pair_occ.shape
    nfreq = cos_weights.shape[0]
    weights = cos_weights.reshape(-1)
    occ_index = pair_occ.T
    virt_index = pair_virt.T
    slot = jnp.pad(partial_target_tile.astype(jnp.float32), (0, SUB * TILE - part)).reshape(SUB, TILE)
    stores = occupied[0], virtual[0]
    first, second = TILE_FIRST
    spans = [(0, first), (first, second)]

    near, far = [], []
    for half, (start, count) in enumerate(spans):
        outs = list(
            tile_first_products(
                occ_index, virt_index, *stores, [] if half else [slot], start, count, terms, blocks, ntau, half == 0
            )
        )
        occ_index, outs[0] = lax.optimization_barrier((occ_index, outs[0]))
        near.append([outs[0]] + [over_tile(outs[s], s, 0, half == 0) for s in range(1, SIDE)])
    strips = list(tau_first_products(occ_index, virt_index, *stores, first + second, TAU_FIRST, terms, ntau))
    strips = over_tau(strips)
    for half in range(2):
        far.append([over_tile(rows, 0, u + 1, half == 0) for u, rows in enumerate(turn(near[half]))])
    weighted = weigh(weights, strips, nfreq)
    piece = lax.all_to_all(weighted, "tile", 0, 0, tiled=True)

    lines = -(-part // TILE)
    stride = lines * TILE
    by_u = [jnp.stack([n[0, first, :lines] for n in near[0]])] + [f[:, first, :lines] for f in far[0]]
    target = jnp.stack(by_u, axis=1).astype(jnp.int32).reshape(-1)
    chi = add_tile_first(target, list(zip(near, far)), spans, stride, ntau)
    times = over_tau(chi)
    spectrum = finish(target, weights, piece, first + second, times, stride, nfreq)
    owned = lax.all_to_all(spectrum, "tile", 0, 0, tiled=True)
    return jnp.transpose(owned, (1, 2, 0, 3))


def solution(mesh):
    in_specs = (
        P("tau", "tile", None, None),
        P("tau", "tile", None, None),
        P(),
        P("tile", None),
        P("tile", None),
        P("tile"),
    )
    out_specs = P(None, "tile", "tau", None)

    return jax.shard_map(body, mesh=mesh, in_specs=in_specs, out_specs=out_specs, check_vma=False)
```

time: 242 us -> 453 us (1.87)
  Pallas kernels: 80.8 us -> 250 us
  waiting for transfers between devices: 94.1 us -> 127 us
  starting transfers between devices: 36.9 us -> 42.8 us
    pallas_call x3 -> x5, Pallas kernels: 42.6 us -> 213 us  [the longest x2 171 us: turn(): pl.pallas_call(turn_kernel, out_shape=[jax.ShapeDtypeStruct(near[0].shape...]
    ppermute x0 -> x12, waiting for transfers between devices: none -> 79.5 us  [over_tile(): lax.ppermute(rows, 'tile', [(i, around(i, s, u, z_first)) for i in range(...]
    ppermute x14, waiting for transfers between devices: 80.1 us -> 47.1 us  [over_tau(): lax.ppermute(strip, 'tau', [(i, partner(i, shift, ntau)) for i in range(n...]
    ppermute x0 -> x12, starting transfers between devices: none -> 20.8 us  [over_tile(): lax.ppermute(rows, 'tile', [(i, around(i, s, u, z_first)) for i in range(...]
    all_to_all x2 -> x0, starting transfers between devices: 12.7 us -> none  [the longest x1 8.17 us: body(): rows = lax.all_to_all(value, 'tile', 0, 0, tiled=True)]
    all_to_all x2 -> x0, waiting for transfers between devices: 7.69 us -> none  [the longest x1 7.69 us: body(): rows = lax.all_to_all(value, 'tile', 0, 0, tiled=True)]
    all_to_all x1, waiting for transfers between devices: 6.3 us -> 0.01 us  [body(): piece = lax.all_to_all(weighted, 'tile', 0, 0, tiled=True)]
  transfers between devices with their start and end apart: 17 -> 27, of which waited for: 12 -> 11; matrix products, arithmetic and copies ran while one was open for 0% -> 1% of each run, Pallas kernels for 23% -> 50%
where the time goes in v1:
time: 453 us; the launch traced here: 452 us
  Pallas kernels  250 us (55%)
  waiting for transfers between devices  127 us (28%)
  starting transfers between devices  42.8 us (9%)
  blocking collectives  21.5 us (5%)
  local copies, waits for them, and re-layouts  10.3 us (2%)
    pallas_call x2, Pallas kernels, turn(): pl.pallas_call(turn_kernel, out_shape=[jax.ShapeDtypeStruct(near[0].shape...  171 us
    ppermute x12, waiting for transfers between devices, over_tile(): lax.ppermute(rows, 'tile', [(i, around(i, s, u, z_first)) for i in range(...  79.5 us
    ppermute x14, waiting for transfers between devices, over_tau(): lax.ppermute(strip, 'tau', [(i, partner(i, shift, ntau)) for i in range(n...  47.1 us
    pallas_call x2, Pallas kernels, tile_first_products(): pl.pallas_call(kernel, out_shape=[jax.ShapeDtypeStruct((SIDE, count + giv...  32.9 us
    pallas_call x1, Pallas kernels, tau_first_products(): pl.pallas_call(kernel, out_shape=[jax.ShapeDtypeStruct((STRIP, count, TIL...  22.4 us
    all_to_all x1, blocking collectives, body(): owned = lax.all_to_all(spectrum, 'tile', 0, 0, tiled=True)  21.5 us
    ppermute x12, starting transfers between devices, over_tile(): lax.ppermute(rows, 'tile', [(i, around(i, s, u, z_first)) for i in range(...  20.8 us
    ppermute x14, starting transfers between devices, over_tau(): lax.ppermute(strip, 'tau', [(i, partner(i, shift, ntau)) for i in range(n...  17.6 us
  transfers between devices with their start and end apart: 27, of which 11 were waited for; matrix products, arithmetic and copies ran while one was open for 1% of the time, Pallas kernels for 50%

profile of v1, /device:TPU:0, one launch (start us, length us, event | category | flops | bytes accessed | tf_op | source)
XLA Modules:
  0.0 452.4 jit_solution(14438325947772662839)
XLA Ops:
  0.0 0.7 convert_element_type.12
  1.3 16.7 %tile_first_products.2 = (f32[4,57,8,128]{3,2,1,0:T(8,128)}, f32[4,57,8,128]{3,2,1,0:T(8,128)}, f32[4,57,8,128]{3,2,1,0:T(8,128)}, f32[4,57,8,128]{3,2,1,0:T(8,128)}) custom-call(s32[16,192]{1,0:T(8,128)} %bitcast.27, s32[16,192]{1,0:T(8,128)} %bitcast.30, bf16[128,128,128]{2,1,0:T(8,128)(2,1)} %bitcast.20, bf16[128,128,128]{2,1,0:T(8,128)(2,1)} %bitcast.23, ...), custom_call_target="tpu_custom_call" | custom-call | tf_op jit(solution)/shard_map/tile_first_products/pallas_call | solution.py:100
  18.0 2.1 collective-permute-start
  20.1 3.6 collective-permute-start.1
  23.7 1.0 collective-permute-start.2
  24.7 16.2 %tile_first_products.3 = (f32[4,56,8,128]{3,2,1,0:T(8,128)}, f32[4,56,8,128]{3,2,1,0:T(8,128)}, f32[4,56,8,128]{3,2,1,0:T(8,128)}, f32[4,56,8,128]{3,2,1,0:T(8,128)}) custom-call(s32[16,192]{1,0:T(8,128)} %bitcast.28, s32[16,192]{1,0:T(8,128)} %bitcast.31, bf16[128,128,128]{2,1,0:T(8,128)(2,1)} %bitcast.21, bf16[128,128,128]{2,1,0:T(8,128)(2,1)} %bitcast.24), custom_call_target="tpu_custom_call" | custom-call | tf_op jit(solution)/shard_map/tile_first_products/pallas_call | solution.py:100
  40.9 22.4 %tau_first_products.1 = (f32[16,80,128]{2,1,0:T(8,128)}, f32[16,80,128]{2,1,0:T(8,128)}, f32[16,80,128]{2,1,0:T(8,128)}, f32[16,80,128]{2,1,0:T(8,128)}, f32[16,...) custom-call(s32[16,192]{1,0:T(8,128)} %bitcast.29, ...), custom_call_target="tpu_custom_call" | custom-call | tf_op jit(solution)/shard_map/tau_first_products/pallas_call | solution.py:147
  63.3 1.7 collective-permute-start.10
  65.0 2.1 collective-permute-start.11
  67.0 15.0 %collective-permute-done.10.refs_6_ = f32[16,80,128]{2,1,0:T(8,128)S(1)} collective-permute-done((f32[16,80,128]{2,1,0:T(8,128)}, f32[16,80,128]{2,1,0:T(8,128)S(1)}, u32[]{:S(2)}, u32[]{:S(2)}) %collective-permute-start.10) | collective-permute-done | bytes 655392 | tf_op jit(solution)/shard_map/ppermute | solution.py:360
  82.1 1.0 collective-permute-start.12
  83.0 11.6 %collective-permute-done.11.refs_7_ = f32[16,80,128]{2,1,0:T(8,128)S(1)} collective-permute-done((f32[16,80,128]{2,1,0:T(8,128)}, f32[16,80,128]{2,1,0:T(8,128)S(1)}, u32[]{:S(2)}, u32[]{:S(2)}) %collective-permute-start.11) | collective-permute-done | bytes 655392 | tf_op jit(solution)/shard_map/ppermute | solution.py:360
  94.6 2.3 collective-permute-start.6
  96.9 0.7 collective-permute-start.7
  98.4 2.8 collective-permute-start.9
  101.2 86.1 %turn.2 = (f32[4,57,8,128]{3,2,1,0:T(8,128)}, f32[4,57,8,128]{3,2,1,0:T(8,128)}, f32[4,57,8,128]{3,2,1,0:T(8,128)}) custom-call(f32[4,57,8,128]{3,2,1,0:T(8,128)} %get-tuple-element.40.refs_0_.refs_1_, f32[4,57,8,128]{3,2,1,0:T(8,128)} %copy-done.3, f32[4,57,8,128]{3,2,1,0:T(8,128)} %copy-done.4, f32[4,57,8,128]{3,2,1,0:T(8,128)} %copy-done.5), custom_call_target="tpu_custom_call" | custom-call | tf_op jit(solution)/shard_map/turn/pallas_call | solution.py:346
  187.2 1.6 collective-permute-start.3
  188.9 1.6 collective-permute-start.13
  190.5 1.6 collective-permute-start.14
  192.0 2.4 collective-permute-start.15
  195.0 6.0 %weigh.1 = f32[16,4,80,128]{3,2,1,0:T(8,128)} custom-call(f32[32]{0:T(128)} %reshape.10.refs_0_.refs_1_, f32[16,80,128]{2,1,0:T(8,128)} %get-tuple-element.50.refs_1_, f32[16,80,128]{2,1,0:T(8,128)} %collective-permute-done.6.refs_2_, f32[16,80,128]{2,1,0:T(8,128)} %collective-permute-done.7.refs_3_, f32[16,80,128]{2,1,0:T(8,128)} %collective-permute-done.8.refs_4_, ...), custom_call_target="tpu_custom_call" | custom-call | tf_op jit(solution)/shard_map/weigh/pallas_call | solution.py:189
  201.0 4.5 all-to-all-start
  205.5 26.5 %collective-permute-done.13.refs_1_.refs_9_ = f32[4,56,8,128]{3,2,1,0:T(8,128)S(1)} collective-permute-done((f32[4,56,8,128]{3,2,1,0:T(8,128)}, f32[4,56,8,128]{3,2,1,0:T(8,128)S(1)}, u32[]{:S(2)}, u32[]{:S(2)}) %collective-permute-start.13) | collective-permute-done | bytes 917536 | tf_op jit(solution)/shard_map/ppermute | solution.py:367
  232.0 21.0 %collective-permute-done.14.refs_2_.refs_10_ = f32[4,56,8,128]{3,2,1,0:T(8,128)S(1)} collective-permute-done((f32[4,56,8,128]{3,2,1,0:T(8,128)}, f32[4,56,8,128]{3,2,1,0:T(8,128)S(1)}, u32[]{:S(2)}, u32[]{:S(2)}) %collective-permute-start.14) | collective-permute-done | bytes 917536 | tf_op jit(solution)/shard_map/ppermute | solution.py:367
  253.0 0.9 copy-done.7
  253.9 0.9 copy-done.8
  254.8 84.6 %turn.3 = (f32[4,56,8,128]{3,2,1,0:T(8,128)}, f32[4,56,8,128]{3,2,1,0:T(8,128)}, f32[4,56,8,128]{3,2,1,0:T(8,128)}) custom-call(f32[4,56,8,128]{3,2,1,0:T(8,128)} %get-tuple-element.58.refs_0_.refs_8_, f32[4,56,8,128]{3,2,1,0:T(8,128)} %copy-done.6, f32[4,56,8,128]{3,2,1,0:T(8,128)} %copy-done.7, f32[4,56,8,128]{3,2,1,0:T(8,128)} %copy-done.8), custom_call_target="tpu_custom_call" | custom-call | tf_op jit(solution)/shard_map/turn/pallas_call | solution.py:346
  339.4 1.1 collective-permute-start.16
  341.0 2.3 collective-permute-start.18
  343.3 3.1 collective-permute-start.4
  346.4 0.7 slice_bitcast_fusion.3
  347.7 0.7 slice_bitcast_fusion.1
  348.4 0.7 slice_bitcast_fusion.2
  349.1 0.7 slice.31
  349.8 16.3 %collective-permute-done.4.refs_6_ = f32[4,57,8,128]{3,2,1,0:T(8,128)S(1)} collective-permute-done((f32[4,57,8,128]{3,2,1,0:T(8,128)}, f32[4,57,8,128]{3,2,1,0:T(8,128)S(1)}, u32[]{:S(2)}, u32[]{:S(2)}) %collective-permute-start.4) | collective-permute-done | bytes 933920 | tf_op jit(solution)/shard_map/ppermute | solution.py:367
  366.1 8.8 %collective-permute-done.5.refs_7_ = f32[4,57,8,128]{3,2,1,0:T(8,128)S(1)} collective-permute-done((f32[4,57,8,128]{3,2,1,0:T(8,128)}, f32[4,57,8,128]{3,2,1,0:T(8,128)S(1)}, u32[]{:S(2)}, u32[]{:S(2)}) %collective-permute-start.5) | collective-permute-done | bytes 933920 | tf_op jit(solution)/shard_map/ppermute | solution.py:367
  375.6 6.3 %collective-permute-done.16.refs_12_ = f32[4,56,8,128]{3,2,1,0:T(8,128)S(1)} collective-permute-done((f32[4,56,8,128]{3,2,1,0:T(8,128)}, f32[4,56,8,128]{3,2,1,0:T(8,128)S(1)}, u32[]{:S(2)}, u32[]{:S(2)}) %collective-permute-start.16) | collective-permute-done | bytes 917536 | tf_op jit(solution)/shard_map/ppermute | solution.py:367
  382.9 1.0 copy-done.13
  383.9 9.8 %add_tile_first.1 = (f32[512,128]{1,0:T(8,128)}, f32[512,128]{1,0:T(8,128)}, f32[512,128]{1,0:T(8,128)}, f32[512,128]{1,0:T(8,128)}, f32[512,128]{1,0:T(8,128)},...) custom-call(s32[4096]{0:T(1024)} %bitcast.18, f32[4,57,8,128]{3,2,1,0:T(8,128)} %get-tuple-element.40.refs_0_.refs_1_, ...), custom_call_target="tpu_custom_call" | custom-call | tf_op jit(solution)/shard_map/add_tile_first/pallas_call | solution.py:245
  393.8 1.2 collective-permute-start.21
  395.0 3.3 collective-permute-start.22
  398.2 1.8 collective-permute-start.24
  400.1 4.3 collective-permute-done.20.refs_5_
  404.4 15.8 %collective-permute-done.21.refs_6_ = f32[512,128]{1,0:T(8,128)S(1)} collective-permute-done((f32[512,128]{1,0:T(8,128)}, f32[512,128]{1,0:T(8,128)S(1)}, u32[]{:S(2)}, u32[]{:S(2)}) %collective-permute-start.21) | collective-permute-done | bytes 262176 | tf_op jit(solution)/shard_map/ppermute | solution.py:360
  420.6 0.9 copy-done
  421.5 7.8 %finish.1 = f32[16,4,32,128]{3,2,1,0:T(8,128)S(1)} custom-call(s32[4096]{0:T(1024)S(1)} %bitcast.19, f32[32]{0:T(128)S(1)} %copy-done.2, f32[16,4,80,128]{3,2,1,0:T(8,128)} %all-to-all-done.refs_2_, f32[512,128]{1,0:T(8,128)S(1)} %copy-done, f32[512,128]{1,0:T(8,128)S(1)} %collective-permute-done.19.refs_4_, f32[512,128]{1,0:T(8,128)S(1)} %collective-permute-done.20.refs_5_, ...), custom_call_target="tpu_custom_call" | custom-call | tf_op jit(solution)/shard_map/finish/pallas_call | solution.py:316
  429.3 21.5 %all_to_all.10 = f32[16,4,32,128]{3,2,1,0:T(8,128)S(1)} all-to-all(f32[16,4,32,128]{3,2,1,0:T(8,128)S(1)} %finish.1), channel_id=1, replica_groups=mesh['tau'=8,'tile'=16] {'tile'}, dimensions={0} | all-to-all | bytes 2097152 | tf_op jit(solution)/shard_map/all_to_all | solution.py:406
  450.8 1.6 copy.7
  (62 shorter events, 5.1 us)
Async XLA Ops:
  18.0 78.9 %collective-permute-start = (f32[4,57,8,128]{3,2,1,0:T(8,128)}, f32[4,57,8,128]{3,2,1,0:T(8,128)S(1)}, u32[]{:S(2)}, u32[]{:S(2)}) collective-permute-start(f32[4,57,8,128]{3,2,1,0:T(8,128)} %get-tuple-element.41), channel_id=1, source_target_pairs={{0,4},{1,5},{2,6},{3,7},{4,8},{5,9},{6,10},{7,11},{8,12},{9,13},{1... | collective-permute-start | bytes 2801672 | tf_op jit(solution)/shard_map/ppermute | solution.py:367
  20.1 77.6 %collective-permute-start.1 = (f32[4,57,8,128]{3,2,1,0:T(8,128)}, f32[4,57,8,128]{3,2,1,0:T(8,128)S(1)}, u32[]{:S(2)}, u32[]{:S(2)}) collective-permute-start(f32[4,57,8,128]{3,2,1,0:T(8,128)} %get-tuple-element.42), channel_id=1, source_target_pairs={{0,8},{1,9},{2,10},{3,11},{4,12},{5,13},{6,14},{7,15},{8,0},{9,1},... | collective-permute-start | bytes 2801672 | tf_op jit(solution)/shard_map/ppermute | solution.py:367
  23.7 74.7 %collective-permute-start.2 = (f32[4,57,8,128]{3,2,1,0:T(8,128)}, f32[4,57,8,128]{3,2,1,0:T(8,128)S(1)}, u32[]{:S(2)}, u32[]{:S(2)}) collective-permute-start(f32[4,57,8,128]{3,2,1,0:T(8,128)} %get-tuple-element.43), channel_id=1, source_target_pairs={{0,12},{1,13},{2,14},{3,15},{4,0},{5,1},{6,2},{7,3},{8,4},{9,5},{1... | collective-permute-start | bytes 2801672 | tf_op jit(solution)/shard_map/ppermute | solution.py:367
  40.9 153.6 %copy-start.16 = (f32[4,8]{1,0:T(4,128)S(1)}, f32[4,8]{1,0:T(4,128)}, u32[]{:S(2)}) copy-start(f32[4,8]{1,0:T(4,128)} %param.8) | copy-start | bytes 388
  63.3 18.8 %collective-permute-start.10 = (f32[16,80,128]{2,1,0:T(8,128)}, f32[16,80,128]{2,1,0:T(8,128)S(1)}, u32[]{:S(2)}, u32[]{:S(2)}) collective-permute-start(f32[16,80,128]{2,1,0:T(8,128)} %get-tuple-element.55), channel_id=1, source_target_pairs={{0,80},{16,64},{32,112},{48,96},{64,16},{80,0},{96,48},{112,32},{1... | collective-permute-start | bytes 1966088 | tf_op jit(solution)/shard_map/ppermute | solution.py:360
  65.0 29.6 %collective-permute-start.11 = (f32[16,80,128]{2,1,0:T(8,128)}, f32[16,80,128]{2,1,0:T(8,128)S(1)}, u32[]{:S(2)}, u32[]{:S(2)}) collective-permute-start(f32[16,80,128]{2,1,0:T(8,128)} %get-tuple-element.56), channel_id=1, source_target_pairs={{0,96},{16,112},{32,0},{48,16},{64,32},{80,48},{96,64},{112,80},{1... | collective-permute-start | bytes 1966088 | tf_op jit(solution)/shard_map/ppermute | solution.py:360
  82.1 112.9 %copy-start.14 = (f32[16,80,128]{2,1,0:T(8,128)}, f32[16,80,128]{2,1,0:T(8,128)S(1)}, u32[]{:S(2)}) copy-start(f32[16,80,128]{2,1,0:T(8,128)S(1)} %collective-permute-done.10.refs_6_) | copy-start | bytes 1966084
  82.1 105.2 %collective-permute-start.12 = (f32[16,80,128]{2,1,0:T(8,128)}, f32[16,80,128]{2,1,0:T(8,128)}, u32[]{:S(2)}, u32[]{:S(2)}) collective-permute-start(f32[16,80,128]{2,1,0:T(8,128)} %get-tuple-element.57), channel_id=1, source_target_pairs={{0,112},{16,96},{32,16},{48,0},{64,48},{80,32},{96,80},{112,64},{1... | collective-permute-start | bytes 1966088 | tf_op jit(solution)/shard_map/ppermute | solution.py:360
  94.6 3.8 copy-start.15
  94.6 94.3 %collective-permute-start.6 = (f32[16,80,128]{2,1,0:T(8,128)}, f32[16,80,128]{2,1,0:T(8,128)}, u32[]{:S(2)}, u32[]{:S(2)}) collective-permute-start(f32[16,80,128]{2,1,0:T(8,128)} %get-tuple-element.51), channel_id=1, source_target_pairs={{0,16},{16,0},{32,48},{48,32},{64,80},{80,64},{96,112},{112,96},{1... | collective-permute-start | bytes 1966088 | tf_op jit(solution)/shard_map/ppermute | solution.py:360
  96.9 4.2 copy-start.3
  96.9 93.5 %collective-permute-start.7 = (f32[16,80,128]{2,1,0:T(8,128)}, f32[16,80,128]{2,1,0:T(8,128)}, u32[]{:S(2)}, u32[]{:S(2)}) collective-permute-start(f32[16,80,128]{2,1,0:T(8,128)} %get-tuple-element.52), channel_id=1, source_target_pairs={{0,32},{16,48},{32,64},{48,80},{64,96},{80,112},{96,0},{112,16},{1... | collective-permute-start | bytes 1966088 | tf_op jit(solution)/shard_map/ppermute | solution.py:360
  97.7 3.5 copy-start.4
  97.7 94.4 %collective-permute-start.8 = (f32[16,80,128]{2,1,0:T(8,128)}, f32[16,80,128]{2,1,0:T(8,128)}, u32[]{:S(2)}, u32[]{:S(2)}) collective-permute-start(f32[16,80,128]{2,1,0:T(8,128)} %get-tuple-element.53), channel_id=1, source_target_pairs={{0,48},{16,32},{32,80},{48,64},{64,112},{80,96},{96,16},{112,0},{1... | collective-permute-start | bytes 1966088 | tf_op jit(solution)/shard_map/ppermute | solution.py:360
  98.4 2.8 copy-start.5
  98.4 96.6 %collective-permute-start.9 = (f32[16,80,128]{2,1,0:T(8,128)}, f32[16,80,128]{2,1,0:T(8,128)}, u32[]{:S(2)}, u32[]{:S(2)}) collective-permute-start(f32[16,80,128]{2,1,0:T(8,128)} %get-tuple-element.54), channel_id=1, source_target_pairs={{0,64},{16,80},{32,96},{48,112},{64,0},{80,16},{96,32},{112,48},{1... | collective-permute-start | bytes 1966088 | tf_op jit(solution)/shard_map/ppermute | solution.py:360
  187.2 159.1 %collective-permute-start.3 = (f32[4,57,8,128]{3,2,1,0:T(8,128)}, f32[4,57,8,128]{3,2,1,0:T(8,128)}, u32[]{:S(2)}, u32[]{:S(2)}) collective-permute-start(f32[4,57,8,128]{3,2,1,0:T(8,128)} %get-tuple-element.44), channel_id=1, source_target_pairs={{0,1},{1,2},{2,3},{3,0},{4,5},{5,6},{6,7},{7,4},{8,9},{9,10},{10,1... | collective-permute-start | bytes 2801672 | tf_op jit(solution)/shard_map/ppermute | solution.py:367
  188.9 43.1 %collective-permute-start.13 = (f32[4,56,8,128]{3,2,1,0:T(8,128)}, f32[4,56,8,128]{3,2,1,0:T(8,128)S(1)}, u32[]{:S(2)}, u32[]{:S(2)}) collective-permute-start(f32[4,56,8,128]{3,2,1,0:T(8,128)} %get-tuple-element.59), channel_id=1, source_target_pairs={{0,1},{1,2},{2,3},{3,0},{4,5},{5,6},{6,7},{7,4},{8,9},{9,10},{10,1... | collective-permute-start | bytes 2752520 | tf_op jit(solution)/shard_map/ppermute | solution.py:367
  190.5 62.5 %collective-permute-start.14 = (f32[4,56,8,128]{3,2,1,0:T(8,128)}, f32[4,56,8,128]{3,2,1,0:T(8,128)S(1)}, u32[]{:S(2)}, u32[]{:S(2)}) collective-permute-start(f32[4,56,8,128]{3,2,1,0:T(8,128)} %get-tuple-element.60), channel_id=1, source_target_pairs={{0,2},{1,3},{2,0},{3,1},{4,6},{5,7},{6,4},{7,5},{8,10},{9,11},{10,... | collective-permute-start | bytes 2752520 | tf_op jit(solution)/shard_map/ppermute | solution.py:367
  192.0 60.9 %collective-permute-start.15 = (f32[4,56,8,128]{3,2,1,0:T(8,128)}, f32[4,56,8,128]{3,2,1,0:T(8,128)S(1)}, u32[]{:S(2)}, u32[]{:S(2)}) collective-permute-start(f32[4,56,8,128]{3,2,1,0:T(8,128)} %get-tuple-element.61), channel_id=1, source_target_pairs={{0,3},{1,0},{2,1},{3,2},{4,7},{5,4},{6,5},{7,6},{8,11},{9,8},{10,9... | collective-permute-start | bytes 2752520 | tf_op jit(solution)/shard_map/ppermute | solution.py:367
  201.0 219.5 %all-to-all-start = ((f32[16,4,80,128]{3,2,1,0:T(8,128)}), f32[16,4,80,128]{3,2,1,0:T(8,128)}, u32[]{:S(2)}, u32[]{:S(2)}) async-start(f32[16,4,80,128]{3,2,1,0:T(8,128)} %weigh.1), calls=%async_computation | async-start | bytes 5242880 | tf_op jit(solution)/shard_map/all_to_all | solution.py:397
  232.0 21.0 %copy-start.6 = (f32[4,56,8,128]{3,2,1,0:T(8,128)}, f32[4,56,8,128]{3,2,1,0:T(8,128)S(1)}, u32[]{:S(2)}) copy-start(f32[4,56,8,128]{3,2,1,0:T(8,128)S(1)} %collective-permute-done.13.refs_1_.refs_9_) | copy-start | bytes 2752516
  253.0 0.9 copy-start.7
  253.9 0.9 copy-start.8
  339.4 42.5 %collective-permute-start.16 = (f32[4,56,8,128]{3,2,1,0:T(8,128)}, f32[4,56,8,128]{3,2,1,0:T(8,128)S(1)}, u32[]{:S(2)}, u32[]{:S(2)}) collective-permute-start(f32[4,56,8,128]{3,2,1,0:T(8,128)} %get-tuple-element.62), channel_id=1, source_target_pairs={{0,4},{1,5},{2,6},{3,7},{4,8},{5,9},{6,10},{7,11},{8,12},{9,13},{1... | collective-permute-start | bytes 2752520 | tf_op jit(solution)/shard_map/ppermute | solution.py:367
  340.5 41.4 %collective-permute-start.17 = (f32[4,56,8,128]{3,2,1,0:T(8,128)}, f32[4,56,8,128]{3,2,1,0:T(8,128)S(1)}, u32[]{:S(2)}, u32[]{:S(2)}) collective-permute-start(f32[4,56,8,128]{3,2,1,0:T(8,128)} %get-tuple-element.63), channel_id=1, source_target_pairs={{0,8},{1,9},{2,10},{3,11},{4,12},{5,13},{6,14},{7,15},{8,0},{9,1},... | collective-permute-start | bytes 2752520 | tf_op jit(solution)/shard_map/ppermute | solution.py:367
  341.0 41.6 %collective-permute-start.18 = (f32[4,56,8,128]{3,2,1,0:T(8,128)}, f32[4,56,8,128]{3,2,1,0:T(8,128)S(1)}, u32[]{:S(2)}, u32[]{:S(2)}) collective-permute-start(f32[4,56,8,128]{3,2,1,0:T(8,128)} %get-tuple-element.64), channel_id=1, source_target_pairs={{0,12},{1,13},{2,14},{3,15},{4,0},{5,1},{6,2},{7,3},{8,4},{9,5},{1... | collective-permute-start | bytes 2752520 | tf_op jit(solution)/shard_map/ppermute | solution.py:367
  343.3 22.8 %collective-permute-start.4 = (f32[4,57,8,128]{3,2,1,0:T(8,128)}, f32[4,57,8,128]{3,2,1,0:T(8,128)S(1)}, u32[]{:S(2)}, u32[]{:S(2)}) collective-permute-start(f32[4,57,8,128]{3,2,1,0:T(8,128)} %get-tuple-element.45), channel_id=1, source_target_pairs={{0,2},{1,3},{2,0},{3,1},{4,6},{5,7},{6,4},{7,5},{8,10},{9,11},{10,... | collective-permute-start | bytes 2801672 | tf_op jit(solution)/shard_map/ppermute | solution.py:367
  346.4 28.6 %collective-permute-start.5 = (f32[4,57,8,128]{3,2,1,0:T(8,128)}, f32[4,57,8,128]{3,2,1,0:T(8,128)S(1)}, u32[]{:S(2)}, u32[]{:S(2)}) collective-permute-start(f32[4,57,8,128]{3,2,1,0:T(8,128)} %get-tuple-element.46), channel_id=1, source_target_pairs={{0,3},{1,0},{2,1},{3,2},{4,7},{5,4},{6,5},{7,6},{8,11},{9,8},{10,9... | collective-permute-start | bytes 2801672 | tf_op jit(solution)/shard_map/ppermute | solution.py:367
  366.1 17.7 %copy-start.9 = (f32[4,57,8,128]{3,2,1,0:T(8,128)}, f32[4,57,8,128]{3,2,1,0:T(8,128)S(1)}, u32[]{:S(2)}) copy-start(f32[4,57,8,128]{3,2,1,0:T(8,128)S(1)} %collective-permute-done.4.refs_6_) | copy-start | bytes 2801668
  375.0 8.9 %copy-start.10 = (f32[4,57,8,128]{3,2,1,0:T(8,128)}, f32[4,57,8,128]{3,2,1,0:T(8,128)S(1)}, u32[]{:S(2)}) copy-start(f32[4,57,8,128]{3,2,1,0:T(8,128)S(1)} %collective-permute-done.5.refs_7_) | copy-start | bytes 2801668
  381.9 2.0 copy-start.11
  381.9 1.0 copy-start.12
  382.9 1.0 copy-start.13
  383.9 36.7 %copy-start.1 = (s32[4,4,2,128]{3,2,1,0:T(2,128)S(1)}, s32[4,4,2,128]{3,2,1,0:T(2,128)}, u32[]{:S(2)}) copy-start(s32[4,4,2,128]{3,2,1,0:T(2,128)} %maximum_convert_fusion) | copy-start | bytes 49156
  383.9 36.7 %copy-start.2 = (f32[32]{0:T(128)S(1)}, f32[32]{0:T(128)}, u32[]{:S(2)}) copy-start(f32[32]{0:T(128)} %reshape.10.refs_0_.refs_1_) | copy-start | bytes 388
  393.7 4.5 %collective-permute-start.19 = (f32[512,128]{1,0:T(8,128)}, f32[512,128]{1,0:T(8,128)S(1)}, u32[]{:S(2)}, u32[]{:S(2)}) collective-permute-start(f32[512,128]{1,0:T(8,128)} %get-tuple-element.66), channel_id=1, source_target_pairs={{0,16},{16,0},{32,48},{48,32},{64,80},{80,64},{96,112},{112,96},{1... | collective-permute-start | bytes 786440 | tf_op jit(solution)/shard_map/ppermute | solution.py:360
  393.7 10.7 %collective-permute-start.20 = (f32[512,128]{1,0:T(8,128)}, f32[512,128]{1,0:T(8,128)S(1)}, u32[]{:S(2)}, u32[]{:S(2)}) collective-permute-start(f32[512,128]{1,0:T(8,128)} %get-tuple-element.67), channel_id=1, source_target_pairs={{0,32},{16,48},{32,64},{48,80},{64,96},{80,112},{96,0},{112,16},{1... | collective-permute-start | bytes 786440 | tf_op jit(solution)/shard_map/ppermute | solution.py:360
  393.8 26.4 %collective-permute-start.21 = (f32[512,128]{1,0:T(8,128)}, f32[512,128]{1,0:T(8,128)S(1)}, u32[]{:S(2)}, u32[]{:S(2)}) collective-permute-start(f32[512,128]{1,0:T(8,128)} %get-tuple-element.68), channel_id=1, source_target_pairs={{0,48},{16,32},{32,80},{48,64},{64,112},{80,96},{96,16},{112,0},{1... | collective-permute-start | bytes 786440 | tf_op jit(solution)/shard_map/ppermute | solution.py:360
  395.0 25.2 %collective-permute-start.22 = (f32[512,128]{1,0:T(8,128)}, f32[512,128]{1,0:T(8,128)S(1)}, u32[]{:S(2)}, u32[]{:S(2)}) collective-permute-start(f32[512,128]{1,0:T(8,128)} %get-tuple-element.69), channel_id=1, source_target_pairs={{0,64},{16,80},{32,96},{48,112},{64,0},{80,16},{96,32},{112,48},{1... | collective-permute-start | bytes 786440 | tf_op jit(solution)/shard_map/ppermute | solution.py:360
  398.2 21.9 %collective-permute-start.23 = (f32[512,128]{1,0:T(8,128)}, f32[512,128]{1,0:T(8,128)S(1)}, u32[]{:S(2)}, u32[]{:S(2)}) collective-permute-start(f32[512,128]{1,0:T(8,128)} %get-tuple-element.70), channel_id=1, source_target_pairs={{0,80},{16,64},{32,112},{48,96},{64,16},{80,0},{96,48},{112,32},{1... | collective-permute-start | bytes 786440 | tf_op jit(solution)/shard_map/ppermute | solution.py:360
  398.2 21.9 %collective-permute-start.24 = (f32[512,128]{1,0:T(8,128)}, f32[512,128]{1,0:T(8,128)S(1)}, u32[]{:S(2)}, u32[]{:S(2)}) collective-permute-start(f32[512,128]{1,0:T(8,128)} %get-tuple-element.71), channel_id=1, source_target_pairs={{0,96},{16,112},{32,0},{48,16},{64,32},{80,48},{96,64},{112,80},{1... | collective-permute-start | bytes 786440 | tf_op jit(solution)/shard_map/ppermute | solution.py:360
  404.4 16.2 %collective-permute-start.25 = (f32[512,128]{1,0:T(8,128)}, f32[512,128]{1,0:T(8,128)S(1)}, u32[]{:S(2)}, u32[]{:S(2)}) collective-permute-start(f32[512,128]{1,0:T(8,128)} %get-tuple-element.72), channel_id=1, source_target_pairs={{0,112},{16,96},{32,16},{48,0},{64,48},{80,32},{96,80},{112,64},{1... | collective-permute-start | bytes 786440 | tf_op jit(solution)/shard_map/ppermute | solution.py:360
  420.5 1.0 copy-start

commit v2 on v1

--- a/solution.py
+++ b/solution.py
@@ -56,66 +56,63 @@
     return (z + dz) % SIDE * SIDE + (y + dy) % SIDE
 
 
-def tile_first_kernel(occ_index, virt_index, occ_far, virt_far, *refs, terms, start, count, ntau, z_first, given):
-    target, outs, (rows, occupied, virtual, arrived, left) = refs[:given], refs[given : given + SIDE], refs[given + SIDE :]
+def tile_first_kernel(occ_index, virt_index, occ_far, virt_far, target, *refs, terms, spans, ntau):
+    n = len(spans) * SIDE
+    outs, halves, (occupied, virtual, arrived, left) = refs[:n], refs[n : n + len(spans)], refs[n + len(spans) :]
     load([(occ_far, occupied), (virt_far, virtual)], arrived)
-    strips, slots = rows.shape[:2]
-    flat = rows.reshape(strips * slots * SUB, TILE)
     offsets = strip_offsets(ntau)
-
-    def step(g, carry):
-        for q in range(SUB):
-            p = g * SUB + q
-            product = product_of(occ_index, virt_index, occupied, virtual, start + p, terms, offsets)
-            for v in range(TILE // SUB):
-                i, h = divmod(v, 2)
-                at = (h * SUB * slots + p) * SUB + i
-                flat[pl.ds(at, SUB, stride=slots * SUB), :] = product[v * SUB : (v + 1) * SUB]
-        return carry
-
-    lax.fori_loop(0, count // SUB, step, 0)
-    for ref in target:
-        for b in range(strips):
-            rows[b, count] = ref[...]
     me = lax.axis_index("tile")
     copies = []
-    for s in range(SIDE):
-        for u in range(SIDE):
-            source = rows.at[around(me, s, u, z_first), pl.ds(0, count + given)]
-            copies.append(pltpu.make_async_copy(source, outs[s].at[u], left.at[s * SIDE + u]))
-    for copy in copies:
-        copy.start()
+    for half, ((start, count), rows) in enumerate(zip(spans, halves)):
+        strips, slots = rows.shape[:2]
+        flat = rows.reshape(strips * slots * SUB, TILE)
+
+        def step(g, carry, start=start, slots=slots, flat=flat):
+            for q in range(SUB):
+                p = g * SUB + q
+                product = product_of(occ_index, virt_index, occupied, virtual, start + p, terms, offsets)
+                for v in range(TILE // SUB):
+                    i, h = divmod(v, 2)
+                    at = (h * SUB * slots + p) * SUB + i
+                    flat[pl.ds(at, SUB, stride=slots * SUB), :] = product[v * SUB : (v + 1) * SUB]
+            return carry
+
+        lax.fori_loop(0, count // SUB, step, 0)
+        if half == 0:
+            for b in range(strips):
+                rows[b, count] = target[...]
+        for s in range(SIDE):
+            for u in range(SIDE):
+                out = outs[half * SIDE + s]
+                source = rows.at[around(me, s, u, half == 0), pl.ds(0, out.shape[1])]
+                copies.append(pltpu.make_async_copy(source, out.at[u], left.at[len(copies)]))
+                copies[-1].start()
     for copy in copies:
         copy.wait()
 
 
-def tile_first_products(occ_index, virt_index, occupied, virtual, targets, start, count, terms, strips, ntau, z_first):
+def tile_first_products(occ_index, virt_index, occupied, virtual, target, spans, terms, strips, ntau):
     far = pl.BlockSpec(memory_space=pltpu.HBM)
     store = pltpu.VMEM(occupied.shape, occupied.dtype)
-    given = len(targets)
 
     def kernel(*refs):
-        tile_first_kernel(*refs, terms=terms, start=start, count=count, ntau=ntau, z_first=z_first, given=given)
-
+        tile_first_kernel(*refs, terms=terms, spans=spans, ntau=ntau)
+
+    sizes = [count + (half == 0) for half, (_, count) in enumerate(spans)]
     return pl.pallas_call(
         kernel,
-        out_shape=[jax.ShapeDtypeStruct((SIDE, count + given, SUB, TILE), jnp.float32)] * SIDE,
+        out_shape=[jax.ShapeDtypeStruct((SIDE, n, SUB, TILE), jnp.float32) for n in sizes for _ in range(SIDE)],
         grid_spec=pltpu.PrefetchScalarGridSpec(
             num_scalar_prefetch=2,
             grid=(1,),
-            in_specs=[far, far] + [pl.BlockSpec((SUB, TILE), lambda g, *_: (0, 0))] * given,
-            out_specs=[far] * SIDE,
-            scratch_shapes=[
-                pltpu.VMEM((strips, count + 1, SUB, TILE), jnp.float32),
-                store,
-                store,
-                pltpu.SemaphoreType.DMA((2,)),
-                pltpu.SemaphoreType.DMA((strips,)),
-            ],
+            in_specs=[far, far, pl.BlockSpec((SUB, TILE), lambda g, *_: (0, 0))],
+            out_specs=[far] * (SIDE * len(spans)),
+            scratch_shapes=[pltpu.VMEM((strips, count + 1, SUB, TILE), jnp.float32) for _, count in spans]
+            + [store, store, pltpu.SemaphoreType.DMA((2,)), pltpu.SemaphoreType.DMA((strips * len(spans),))],
         ),
         compiler_params=pltpu.CompilerParams(vmem_limit_bytes=60 * 2**20),
         name="tile_first_products",
-    )(occ_index, virt_index, occupied, virtual, *targets)
+    )(occ_index, virt_index, occupied, virtual, target)
 
 
 def tau_first_kernel(occ_index, virt_index, occ_far, virt_far, *refs, terms, start, ntau):
@@ -330,14 +327,20 @@
 
 
 def turn_kernel(*refs):
-    near, outs, arrived = refs[:SIDE], refs[SIDE:-1], refs[-1]
-    copies = []
+    near, outs, held, arrived, left = refs[:SIDE], refs[SIDE:-3], *refs[-3:]
+    inward = []
     for u in range(1, SIDE):
         for s in range(SIDE):
-            copies.append(pltpu.make_async_copy(near[s].at[u], outs[u - 1].at[s], arrived.at[(u - 1) * SIDE + s]))
-    for copy in copies:
+            at = (u - 1) * SIDE + s
+            inward.append(pltpu.make_async_copy(near[s].at[u], held.at[u - 1, s], arrived.at[at]))
+    outward = [pltpu.make_async_copy(held.at[u], out, left.at[u]) for u, out in enumerate(outs)]
+    for copy in inward:
         copy.start()
-    for copy in copies:
+    for u, copy in enumerate(outward):
+        for s in range(SIDE):
+            inward[u * SIDE + s].wait()
+        copy.start()
+    for copy in outward:
         copy.wait()
 
 
@@ -348,7 +351,11 @@
         out_shape=[jax.ShapeDtypeStruct(near[0].shape, jnp.float32)] * (SIDE - 1),
         in_specs=[anywhere] * SIDE,
         out_specs=[anywhere] * (SIDE - 1),
-        scratch_shapes=[pltpu.SemaphoreType.DMA((SIDE * (SIDE - 1),))],
+        scratch_shapes=[
+            pltpu.VMEM((SIDE - 1, *near[0].shape), jnp.float32),
+            pltpu.SemaphoreType.DMA((SIDE * (SIDE - 1),)),
+            pltpu.SemaphoreType.DMA((SIDE - 1,)),
+        ],
         compiler_params=pltpu.CompilerParams(vmem_limit_bytes=60 * 2**20),
         name="turn",
     )(*near)
@@ -381,14 +388,11 @@
     spans = [(0, first), (first, second)]
 
     near, far = [], []
-    for half, (start, count) in enumerate(spans):
-        outs = list(
-            tile_first_products(
-                occ_index, virt_index, *stores, [] if half else [slot], start, count, terms, blocks, ntau, half == 0
-            )
-        )
-        occ_index, outs[0] = lax.optimization_barrier((occ_index, outs[0]))
-        near.append([outs[0]] + [over_tile(outs[s], s, 0, half == 0) for s in range(1, SIDE)])
+    outs = list(tile_first_products(occ_index, virt_index, *stores, slot, spans, terms, blocks, ntau))
+    occ_index, outs[0] = lax.optimization_barrier((occ_index, outs[0]))
+    for half in range(2):
+        mine, *others = outs[half * SIDE : (half + 1) * SIDE]
+        near.append([mine] + [over_tile(rows, s + 1, 0, half == 0) for s, rows in enumerate(others)])
     strips = list(tau_first_products(occ_index, virt_index, *stores, first + second, TAU_FIRST, terms, ntau))
     strips = over_tau(strips)
     for half in range(2):

time: 453 us -> 301 us (0.66)
  Pallas kernels: 250 us -> 79.8 us
  waiting for transfers between devices: 127 us -> 139 us
    pallas_call x2, Pallas kernels: 171 us -> 5.97 us  [turn(): pl.pallas_call(turn_kernel, out_shape=[jax.ShapeDtypeStruct(near[0].shape...]
    ppermute x14, waiting for transfers between devices: 47.1 us -> 77.6 us  [over_tau(): lax.ppermute(strip, 'tau', [(i, partner(i, shift, ntau)) for i in range(n...]
    ppermute x12, waiting for transfers between devices: 79.5 us -> 61.7 us  [over_tile(): lax.ppermute(rows, 'tile', [(i, around(i, s, u, z_first)) for i in range(...]
    pallas_call x2 -> x1, Pallas kernels: 32.9 us -> 27.7 us  [tile_first_products(): pl.pallas_call(kernel, out_shape=[jax.ShapeDtypeStruct((SIDE, n, SUB, TIL...]
  transfers between devices with their start and end apart: 27 -> 27, of which waited for: 11 -> 15; matrix products, arithmetic and copies ran while one was open for 1% -> 2% of each run, Pallas kernels for 50% -> 15%
where the time goes in v2:
time: 301 us; the launch traced here: 299 us
  waiting for transfers between devices  139 us (46%)
  Pallas kernels  79.8 us (27%)
  starting transfers between devices  45.6 us (15%)
  blocking collectives  23.8 us (8%)
  local copies, waits for them, and re-layouts  9.44 us (3%)
    ppermute x14, waiting for transfers between devices, over_tau(): lax.ppermute(strip, 'tau', [(i, partner(i, shift, ntau)) for i in range(n...  77.6 us
    ppermute x12, waiting for transfers between devices, over_tile(): lax.ppermute(rows, 'tile', [(i, around(i, s, u, z_first)) for i in range(...  61.7 us
    pallas_call x1, Pallas kernels, tile_first_products(): pl.pallas_call(kernel, out_shape=[jax.ShapeDtypeStruct((SIDE, n, SUB, TIL...  27.7 us
    ppermute x12, starting transfers between devices, over_tile(): lax.ppermute(rows, 'tile', [(i, around(i, s, u, z_first)) for i in range(...  24.7 us
    all_to_all x1, blocking collectives, body(): owned = lax.all_to_all(spectrum, 'tile', 0, 0, tiled=True)  23.8 us
    pallas_call x1, Pallas kernels, tau_first_products(): pl.pallas_call(kernel, out_shape=[jax.ShapeDtypeStruct((STRIP, count, TIL...  22.5 us
    ppermute x14, starting transfers between devices, over_tau(): lax.ppermute(strip, 'tau', [(i, partner(i, shift, ntau)) for i in range(n...  15.8 us
    pallas_call x1, Pallas kernels, add_tile_first(): pl.pallas_call(kernel, out_shape=[jax.ShapeDtypeStruct((tiles, TILE), jnp...  9.8 us
  transfers between devices with their start and end apart: 27, of which 15 were waited for; matrix products, arithmetic and copies ran while one was open for 2% of the time, Pallas kernels for 15%

profile of v2, /device:TPU:0, one launch (start us, length us, event | category | flops | bytes accessed | tf_op | source)
XLA Modules:
  0.0 299.5 jit_solution(3337644214923223016)
XLA Ops:
  1.3 27.7 %tile_first_products.1 = (f32[4,57,8,128]{3,2,1,0:T(8,128)}, f32[4,57,8,128]{3,2,1,0:T(8,128)}, f32[4,57,8,128]{3,2,1,0:T(8,128)}, f32[4,57,8,128]{3,2,1,0:T(8,1...) custom-call(s32[16,192]{1,0:T(8,128)} %bitcast.25, ...), custom_call_target="tpu_custom_call" | custom-call | tf_op jit(solution)/shard_map/tile_first_products/pallas_call | solution.py:102
  29.0 2.1 collective-permute-start
  31.1 3.6 %collective-permute-start.1 = (f32[4,57,8,128]{3,2,1,0:T(8,128)}, f32[4,57,8,128]{3,2,1,0:T(8,128)S(1)}, u32[]{:S(2)}, u32[]{:S(2)}) collective-permute-start(f32[4,57,8,128]{3,2,1,0:T(8,128)} %get-tuple-element.40), channel_id=1, source_target_pairs={{0,8},{1,9},{2,10},{3,11},{4,12},{5,13},{6,14},{7,15},{8,0},{9,1},... | collective-permute-start | bytes 2801672 | tf_op jit(solution)/shard_map/ppermute | solution.py:374
  34.7 1.0 collective-permute-start.2
  35.7 22.5 %tau_first_products.1 = (f32[16,80,128]{2,1,0:T(8,128)}, f32[16,80,128]{2,1,0:T(8,128)}, f32[16,80,128]{2,1,0:T(8,128)}, f32[16,80,128]{2,1,0:T(8,128)}, f32[16,...) custom-call(s32[16,192]{1,0:T(8,128)} %bitcast.26, ...), custom_call_target="tpu_custom_call" | custom-call | tf_op jit(solution)/shard_map/tau_first_products/pallas_call | solution.py:144
  58.3 1.0 collective-permute-start.10
  59.2 1.9 collective-permute-start.11
  61.1 15.9 %collective-permute-done.10.refs_6_ = f32[16,80,128]{2,1,0:T(8,128)S(1)} collective-permute-done((f32[16,80,128]{2,1,0:T(8,128)}, f32[16,80,128]{2,1,0:T(8,128)S(1)}, u32[]{:S(2)}, u32[]{:S(2)}) %collective-permute-start.10) | collective-permute-done | bytes 655392 | tf_op jit(solution)/shard_map/ppermute | solution.py:367
  77.6 11.6 %collective-permute-done.11.refs_7_ = f32[16,80,128]{2,1,0:T(8,128)S(1)} collective-permute-done((f32[16,80,128]{2,1,0:T(8,128)}, f32[16,80,128]{2,1,0:T(8,128)S(1)}, u32[]{:S(2)}, u32[]{:S(2)}) %collective-permute-start.11) | collective-permute-done | bytes 655392 | tf_op jit(solution)/shard_map/ppermute | solution.py:367
  89.2 1.8 collective-permute-start.6
  91.0 0.8 collective-permute-start.7
  92.4 2.8 collective-permute-start.9
  95.2 3.0 turn.2
  98.2 7.1 %collective-permute-done.12.refs_8_ = f32[16,80,128]{2,1,0:T(8,128)} collective-permute-done((f32[16,80,128]{2,1,0:T(8,128)}, f32[16,80,128]{2,1,0:T(8,128)}, u32[]{:S(2)}, u32[]{:S(2)}) %collective-permute-start.12) | collective-permute-done | bytes 655392 | tf_op jit(solution)/shard_map/ppermute | solution.py:367
  105.4 1.6 collective-permute-start.3
  106.9 1.6 collective-permute-start.13
  108.5 1.7 collective-permute-done.7.refs_3_
  110.2 3.2 %collective-permute-start.14 = (f32[4,56,8,128]{3,2,1,0:T(8,128)}, f32[4,56,8,128]{3,2,1,0:T(8,128)S(1)}, u32[]{:S(2)}, u32[]{:S(2)}) collective-permute-start(f32[4,56,8,128]{3,2,1,0:T(8,128)} %get-tuple-element.56), channel_id=1, source_target_pairs={{0,2},{1,3},{2,0},{3,1},{4,6},{5,7},{6,4},{7,5},{8,10},{9,11},{10,... | collective-permute-start | bytes 2752520 | tf_op jit(solution)/shard_map/ppermute | solution.py:374
  113.4 9.1 %collective-permute-done.8.refs_4_ = f32[16,80,128]{2,1,0:T(8,128)} collective-permute-done((f32[16,80,128]{2,1,0:T(8,128)}, f32[16,80,128]{2,1,0:T(8,128)}, u32[]{:S(2)}, u32[]{:S(2)}) %collective-permute-start.8) | collective-permute-done | bytes 655392 | tf_op jit(solution)/shard_map/ppermute | solution.py:367
  122.4 3.0 %collective-permute-start.15 = (f32[4,56,8,128]{3,2,1,0:T(8,128)}, f32[4,56,8,128]{3,2,1,0:T(8,128)S(1)}, u32[]{:S(2)}, u32[]{:S(2)}) collective-permute-start(f32[4,56,8,128]{3,2,1,0:T(8,128)} %get-tuple-element.57), channel_id=1, source_target_pairs={{0,3},{1,0},{2,1},{3,2},{4,7},{5,4},{6,5},{7,6},{8,11},{9,8},{10,9... | collective-permute-start | bytes 2752520 | tf_op jit(solution)/shard_map/ppermute | solution.py:374
  126.1 11.7 %collective-permute-done.9.refs_5_ = f32[16,80,128]{2,1,0:T(8,128)} collective-permute-done((f32[16,80,128]{2,1,0:T(8,128)}, f32[16,80,128]{2,1,0:T(8,128)}, u32[]{:S(2)}, u32[]{:S(2)}) %collective-permute-start.9) | collective-permute-done | bytes 655392 | tf_op jit(solution)/shard_map/ppermute | solution.py:367
  137.8 6.0 %weigh.1 = f32[16,4,80,128]{3,2,1,0:T(8,128)} custom-call(f32[32]{0:T(128)} %reshape.10.refs_0_.refs_1_, f32[16,80,128]{2,1,0:T(8,128)} %get-tuple-element.46.refs_1_, f32[16,80,128]{2,1,0:T(8,128)} %collective-permute-done.6.refs_2_, f32[16,80,128]{2,1,0:T(8,128)} %collective-permute-done.7.refs_3_, f32[16,80,128]{2,1,0:T(8,128)} %collective-permute-done.8.refs_4_, ...), custom_call_target="tpu_custom_call" | custom-call | tf_op jit(solution)/shard_map/weigh/pallas_call | solution.py:186
  143.8 5.1 %all-to-all-start = ((f32[16,4,80,128]{3,2,1,0:T(8,128)}), f32[16,4,80,128]{3,2,1,0:T(8,128)}, u32[]{:S(2)}, u32[]{:S(2)}) async-start(f32[16,4,80,128]{3,2,1,0:T(8,128)} %weigh.1), calls=%async_computation | async-start | bytes 5242880 | tf_op jit(solution)/shard_map/all_to_all | solution.py:401
  148.9 22.1 %collective-permute-done.14.refs_2_.refs_10_ = f32[4,56,8,128]{3,2,1,0:T(8,128)S(1)} collective-permute-done((f32[4,56,8,128]{3,2,1,0:T(8,128)}, f32[4,56,8,128]{3,2,1,0:T(8,128)S(1)}, u32[]{:S(2)}, u32[]{:S(2)}) %collective-permute-start.14) | collective-permute-done | bytes 917536 | tf_op jit(solution)/shard_map/ppermute | solution.py:374
  171.0 0.9 copy-done.7
  172.2 3.0 turn.3
  175.2 1.1 collective-permute-start.16
  176.8 2.3 collective-permute-start.18
  179.1 4.8 %collective-permute-start.4 = (f32[4,57,8,128]{3,2,1,0:T(8,128)}, f32[4,57,8,128]{3,2,1,0:T(8,128)S(1)}, u32[]{:S(2)}, u32[]{:S(2)}) collective-permute-start(f32[4,57,8,128]{3,2,1,0:T(8,128)} %get-tuple-element.43), channel_id=1, source_target_pairs={{0,2},{1,3},{2,0},{3,1},{4,6},{5,7},{6,4},{7,5},{8,10},{9,11},{10,... | collective-permute-start | bytes 2801672 | tf_op jit(solution)/shard_map/ppermute | solution.py:374
  183.9 0.7 slice_bitcast_fusion.3
  186.6 0.7 slice.31
  187.3 29.8 %collective-permute-done.4.refs_6_ = f32[4,57,8,128]{3,2,1,0:T(8,128)S(1)} collective-permute-done((f32[4,57,8,128]{3,2,1,0:T(8,128)}, f32[4,57,8,128]{3,2,1,0:T(8,128)S(1)}, u32[]{:S(2)}, u32[]{:S(2)}) %collective-permute-start.4) | collective-permute-done | bytes 933920 | tf_op jit(solution)/shard_map/ppermute | solution.py:374
  217.1 6.3 %collective-permute-done.5.refs_7_ = f32[4,57,8,128]{3,2,1,0:T(8,128)S(1)} collective-permute-done((f32[4,57,8,128]{3,2,1,0:T(8,128)}, f32[4,57,8,128]{3,2,1,0:T(8,128)S(1)}, u32[]{:S(2)}, u32[]{:S(2)}) %collective-permute-start.5) | collective-permute-done | bytes 933920 | tf_op jit(solution)/shard_map/ppermute | solution.py:374
  224.1 3.5 %collective-permute-done.18.refs_14_ = f32[4,56,8,128]{3,2,1,0:T(8,128)S(1)} collective-permute-done((f32[4,56,8,128]{3,2,1,0:T(8,128)}, f32[4,56,8,128]{3,2,1,0:T(8,128)S(1)}, u32[]{:S(2)}, u32[]{:S(2)}) %collective-permute-start.18) | collective-permute-done | bytes 917536 | tf_op jit(solution)/shard_map/ppermute | solution.py:374
  227.6 1.0 copy-done.13
  228.6 9.8 %add_tile_first.1 = (f32[512,128]{1,0:T(8,128)}, f32[512,128]{1,0:T(8,128)}, f32[512,128]{1,0:T(8,128)}, f32[512,128]{1,0:T(8,128)}, f32[512,128]{1,0:T(8,128)},...) custom-call(s32[4096]{0:T(1024)} %bitcast.18, f32[4,57,8,128]{3,2,1,0:T(8,128)} %get-tuple-element.38.refs_0_.refs_1_, ...), custom_call_target="tpu_custom_call" | custom-call | tf_op jit(solution)/shard_map/add_tile_first/pallas_call | solution.py:242
  238.6 0.8 collective-permute-start.21
  239.5 3.5 %collective-permute-start.22 = (f32[512,128]{1,0:T(8,128)}, f32[512,128]{1,0:T(8,128)S(1)}, u32[]{:S(2)}, u32[]{:S(2)}) collective-permute-start(f32[512,128]{1,0:T(8,128)} %get-tuple-element.65), channel_id=1, source_target_pairs={{0,64},{16,80},{32,96},{48,112},{64,0},{80,16},{96,32},{112,48},{1... | collective-permute-start | bytes 786440 | tf_op jit(solution)/shard_map/ppermute | solution.py:367
  243.0 1.9 collective-permute-start.24
  244.8 4.2 %collective-permute-done.20.refs_5_ = f32[512,128]{1,0:T(8,128)S(1)} collective-permute-done((f32[512,128]{1,0:T(8,128)}, f32[512,128]{1,0:T(8,128)S(1)}, u32[]{:S(2)}, u32[]{:S(2)}) %collective-permute-start.20) | collective-permute-done | bytes 262176 | tf_op jit(solution)/shard_map/ppermute | solution.py:367
  249.1 5.0 %collective-permute-done.21.refs_6_ = f32[512,128]{1,0:T(8,128)S(1)} collective-permute-done((f32[512,128]{1,0:T(8,128)}, f32[512,128]{1,0:T(8,128)S(1)}, u32[]{:S(2)}, u32[]{:S(2)}) %collective-permute-start.21) | collective-permute-done | bytes 262176 | tf_op jit(solution)/shard_map/ppermute | solution.py:367
  254.1 5.8 %collective-permute-done.22.refs_7_ = f32[512,128]{1,0:T(8,128)S(1)} collective-permute-done((f32[512,128]{1,0:T(8,128)}, f32[512,128]{1,0:T(8,128)S(1)}, u32[]{:S(2)}, u32[]{:S(2)}) %collective-permute-start.22) | collective-permute-done | bytes 262176 | tf_op jit(solution)/shard_map/ppermute | solution.py:367
  259.9 4.5 %collective-permute-done.23.refs_8_ = f32[512,128]{1,0:T(8,128)S(1)} collective-permute-done((f32[512,128]{1,0:T(8,128)}, f32[512,128]{1,0:T(8,128)S(1)}, u32[]{:S(2)}, u32[]{:S(2)}) %collective-permute-start.23) | collective-permute-done | bytes 262176 | tf_op jit(solution)/shard_map/ppermute | solution.py:367
  264.5 0.9 collective-permute-done.25.refs_10_
  265.4 0.9 copy-done
  266.3 7.8 %finish.1 = f32[16,4,32,128]{3,2,1,0:T(8,128)S(1)} custom-call(s32[4096]{0:T(1024)S(1)} %bitcast.19, f32[32]{0:T(128)S(1)} %copy-done.2, f32[16,4,80,128]{3,2,1,0:T(8,128)} %all-to-all-done.refs_2_, f32[512,128]{1,0:T(8,128)S(1)} %copy-done, f32[512,128]{1,0:T(8,128)S(1)} %collective-permute-done.19.refs_4_, f32[512,128]{1,0:T(8,128)S(1)} %collective-permute-done.20.refs_5_, ...), custom_call_target="tpu_custom_call" | custom-call | tf_op jit(solution)/shard_map/finish/pallas_call | solution.py:313
  274.1 23.8 %all_to_all.10 = f32[16,4,32,128]{3,2,1,0:T(8,128)S(1)} all-to-all(f32[16,4,32,128]{3,2,1,0:T(8,128)S(1)} %finish.1), channel_id=1, replica_groups=mesh['tau'=8,'tile'=16] {'tile'}, dimensions={0} | all-to-all | bytes 2097152 | tf_op jit(solution)/shard_map/all_to_all | solution.py:410
  297.9 1.6 copy.7
  (61 shorter events, 6.8 us)
Async XLA Ops:
  29.0 62.0 %collective-permute-start = (f32[4,57,8,128]{3,2,1,0:T(8,128)}, f32[4,57,8,128]{3,2,1,0:T(8,128)S(1)}, u32[]{:S(2)}, u32[]{:S(2)}) collective-permute-start(f32[4,57,8,128]{3,2,1,0:T(8,128)} %get-tuple-element.39), channel_id=1, source_target_pairs={{0,4},{1,5},{2,6},{3,7},{4,8},{5,9},{6,10},{7,11},{8,12},{9,13},{1... | collective-permute-start | bytes 2801672 | tf_op jit(solution)/shard_map/ppermute | solution.py:374
  31.1 60.7 %collective-permute-start.1 = (f32[4,57,8,128]{3,2,1,0:T(8,128)}, f32[4,57,8,128]{3,2,1,0:T(8,128)S(1)}, u32[]{:S(2)}, u32[]{:S(2)}) collective-permute-start(f32[4,57,8,128]{3,2,1,0:T(8,128)} %get-tuple-element.40), channel_id=1, source_target_pairs={{0,8},{1,9},{2,10},{3,11},{4,12},{5,13},{6,14},{7,15},{8,0},{9,1},... | collective-permute-start | bytes 2801672 | tf_op jit(solution)/shard_map/ppermute | solution.py:374
  34.7 57.8 %collective-permute-start.2 = (f32[4,57,8,128]{3,2,1,0:T(8,128)}, f32[4,57,8,128]{3,2,1,0:T(8,128)S(1)}, u32[]{:S(2)}, u32[]{:S(2)}) collective-permute-start(f32[4,57,8,128]{3,2,1,0:T(8,128)} %get-tuple-element.41), channel_id=1, source_target_pairs={{0,12},{1,13},{2,14},{3,15},{4,0},{5,1},{6,2},{7,3},{8,4},{9,5},{1... | collective-permute-start | bytes 2801672 | tf_op jit(solution)/shard_map/ppermute | solution.py:374
  35.7 89.7 %copy-start.16 = (f32[4,8]{1,0:T(4,128)S(1)}, f32[4,8]{1,0:T(4,128)}, u32[]{:S(2)}) copy-start(f32[4,8]{1,0:T(4,128)} %param.8) | copy-start | bytes 388
  58.3 18.8 %collective-permute-start.10 = (f32[16,80,128]{2,1,0:T(8,128)}, f32[16,80,128]{2,1,0:T(8,128)S(1)}, u32[]{:S(2)}, u32[]{:S(2)}) collective-permute-start(f32[16,80,128]{2,1,0:T(8,128)} %get-tuple-element.51), channel_id=1, source_target_pairs={{0,80},{16,64},{32,112},{48,96},{64,16},{80,0},{96,48},{112,32},{1... | collective-permute-start | bytes 1966088 | tf_op jit(solution)/shard_map/ppermute | solution.py:367
  59.2 30.0 %collective-permute-start.11 = (f32[16,80,128]{2,1,0:T(8,128)}, f32[16,80,128]{2,1,0:T(8,128)S(1)}, u32[]{:S(2)}, u32[]{:S(2)}) collective-permute-start(f32[16,80,128]{2,1,0:T(8,128)} %get-tuple-element.52), channel_id=1, source_target_pairs={{0,96},{16,112},{32,0},{48,16},{64,32},{80,48},{96,64},{112,80},{1... | collective-permute-start | bytes 1966088 | tf_op jit(solution)/shard_map/ppermute | solution.py:367
  77.0 60.8 %copy-start.14 = (f32[16,80,128]{2,1,0:T(8,128)}, f32[16,80,128]{2,1,0:T(8,128)S(1)}, u32[]{:S(2)}) copy-start(f32[16,80,128]{2,1,0:T(8,128)S(1)} %collective-permute-done.10.refs_6_) | copy-start | bytes 1966084
  77.0 28.3 %collective-permute-start.12 = (f32[16,80,128]{2,1,0:T(8,128)}, f32[16,80,128]{2,1,0:T(8,128)}, u32[]{:S(2)}, u32[]{:S(2)}) collective-permute-start(f32[16,80,128]{2,1,0:T(8,128)} %get-tuple-element.53), channel_id=1, source_target_pairs={{0,112},{16,96},{32,16},{48,0},{64,48},{80,32},{96,80},{112,64},{1... | collective-permute-start | bytes 1966088 | tf_op jit(solution)/shard_map/ppermute | solution.py:367
  89.2 3.2 %copy-start.15 = (f32[16,80,128]{2,1,0:T(8,128)}, f32[16,80,128]{2,1,0:T(8,128)S(1)}, u32[]{:S(2)}) copy-start(f32[16,80,128]{2,1,0:T(8,128)S(1)} %collective-permute-done.11.refs_7_) | copy-start | bytes 1966084
  89.2 17.7 %collective-permute-start.6 = (f32[16,80,128]{2,1,0:T(8,128)}, f32[16,80,128]{2,1,0:T(8,128)}, u32[]{:S(2)}, u32[]{:S(2)}) collective-permute-start(f32[16,80,128]{2,1,0:T(8,128)} %get-tuple-element.47), channel_id=1, source_target_pairs={{0,16},{16,0},{32,48},{48,32},{64,80},{80,64},{96,112},{112,96},{1... | collective-permute-start | bytes 1966088 | tf_op jit(solution)/shard_map/ppermute | solution.py:367
  91.0 4.2 %copy-start.3 = (f32[4,57,8,128]{3,2,1,0:T(8,128)}, f32[4,57,8,128]{3,2,1,0:T(8,128)S(1)}, u32[]{:S(2)}) copy-start(f32[4,57,8,128]{3,2,1,0:T(8,128)S(1)} %collective-permute-done.refs_1_.refs_2_) | copy-start | bytes 2801668
  91.0 19.1 %collective-permute-start.7 = (f32[16,80,128]{2,1,0:T(8,128)}, f32[16,80,128]{2,1,0:T(8,128)}, u32[]{:S(2)}, u32[]{:S(2)}) collective-permute-start(f32[16,80,128]{2,1,0:T(8,128)} %get-tuple-element.48), channel_id=1, source_target_pairs={{0,32},{16,48},{32,64},{48,80},{64,96},{80,112},{96,0},{112,16},{1... | collective-permute-start | bytes 1966088 | tf_op jit(solution)/shard_map/ppermute | solution.py:367
  91.8 3.4 %copy-start.4 = (f32[4,57,8,128]{3,2,1,0:T(8,128)}, f32[4,57,8,128]{3,2,1,0:T(8,128)S(1)}, u32[]{:S(2)}) copy-start(f32[4,57,8,128]{3,2,1,0:T(8,128)S(1)} %collective-permute-done.1.refs_2_.refs_3_) | copy-start | bytes 2801668
  91.8 30.6 %collective-permute-start.8 = (f32[16,80,128]{2,1,0:T(8,128)}, f32[16,80,128]{2,1,0:T(8,128)}, u32[]{:S(2)}, u32[]{:S(2)}) collective-permute-start(f32[16,80,128]{2,1,0:T(8,128)} %get-tuple-element.49), channel_id=1, source_target_pairs={{0,48},{16,32},{32,80},{48,64},{64,112},{80,96},{96,16},{112,0},{1... | collective-permute-start | bytes 1966088 | tf_op jit(solution)/shard_map/ppermute | solution.py:367
  92.4 2.8 copy-start.5
  92.4 45.4 %collective-permute-start.9 = (f32[16,80,128]{2,1,0:T(8,128)}, f32[16,80,128]{2,1,0:T(8,128)}, u32[]{:S(2)}, u32[]{:S(2)}) collective-permute-start(f32[16,80,128]{2,1,0:T(8,128)} %get-tuple-element.50), channel_id=1, source_target_pairs={{0,64},{16,80},{32,96},{48,112},{64,0},{80,16},{96,32},{112,48},{1... | collective-permute-start | bytes 1966088 | tf_op jit(solution)/shard_map/ppermute | solution.py:367
  105.4 78.5 %collective-permute-start.3 = (f32[4,57,8,128]{3,2,1,0:T(8,128)}, f32[4,57,8,128]{3,2,1,0:T(8,128)}, u32[]{:S(2)}, u32[]{:S(2)}) collective-permute-start(f32[4,57,8,128]{3,2,1,0:T(8,128)} %get-tuple-element.42), channel_id=1, source_target_pairs={{0,1},{1,2},{2,3},{3,0},{4,5},{5,6},{6,7},{7,4},{8,9},{9,10},{10,1... | collective-permute-start | bytes 2801672 | tf_op jit(solution)/shard_map/ppermute | solution.py:374
  106.9 42.0 %collective-permute-start.13 = (f32[4,56,8,128]{3,2,1,0:T(8,128)}, f32[4,56,8,128]{3,2,1,0:T(8,128)S(1)}, u32[]{:S(2)}, u32[]{:S(2)}) collective-permute-start(f32[4,56,8,128]{3,2,1,0:T(8,128)} %get-tuple-element.55), channel_id=1, source_target_pairs={{0,1},{1,2},{2,3},{3,0},{4,5},{5,6},{6,7},{7,4},{8,9},{9,10},{10,1... | collective-permute-start | bytes 2752520 | tf_op jit(solution)/shard_map/ppermute | solution.py:374
  110.2 60.8 %collective-permute-start.14 = (f32[4,56,8,128]{3,2,1,0:T(8,128)}, f32[4,56,8,128]{3,2,1,0:T(8,128)S(1)}, u32[]{:S(2)}, u32[]{:S(2)}) collective-permute-start(f32[4,56,8,128]{3,2,1,0:T(8,128)} %get-tuple-element.56), channel_id=1, source_target_pairs={{0,2},{1,3},{2,0},{3,1},{4,6},{5,7},{6,4},{7,5},{8,10},{9,11},{10,... | collective-permute-start | bytes 2752520 | tf_op jit(solution)/shard_map/ppermute | solution.py:374
  122.4 48.6 %collective-permute-start.15 = (f32[4,56,8,128]{3,2,1,0:T(8,128)}, f32[4,56,8,128]{3,2,1,0:T(8,128)S(1)}, u32[]{:S(2)}, u32[]{:S(2)}) collective-permute-start(f32[4,56,8,128]{3,2,1,0:T(8,128)} %get-tuple-element.57), channel_id=1, source_target_pairs={{0,3},{1,0},{2,1},{3,2},{4,7},{5,4},{6,5},{7,6},{8,11},{9,8},{10,9... | collective-permute-start | bytes 2752520 | tf_op jit(solution)/shard_map/ppermute | solution.py:374
  143.8 121.6 %all-to-all-start = ((f32[16,4,80,128]{3,2,1,0:T(8,128)}), f32[16,4,80,128]{3,2,1,0:T(8,128)}, u32[]{:S(2)}, u32[]{:S(2)}) async-start(f32[16,4,80,128]{3,2,1,0:T(8,128)} %weigh.1), calls=%async_computation | async-start | bytes 5242880 | tf_op jit(solution)/shard_map/all_to_all | solution.py:401
  148.9 22.1 %copy-start.6 = (f32[4,56,8,128]{3,2,1,0:T(8,128)}, f32[4,56,8,128]{3,2,1,0:T(8,128)S(1)}, u32[]{:S(2)}) copy-start(f32[4,56,8,128]{3,2,1,0:T(8,128)S(1)} %collective-permute-done.13.refs_1_.refs_9_) | copy-start | bytes 2752516
  171.0 0.9 copy-start.7
  171.0 1.2 copy-start.8
  175.2 48.9 %collective-permute-start.16 = (f32[4,56,8,128]{3,2,1,0:T(8,128)}, f32[4,56,8,128]{3,2,1,0:T(8,128)S(1)}, u32[]{:S(2)}, u32[]{:S(2)}) collective-permute-start(f32[4,56,8,128]{3,2,1,0:T(8,128)} %get-tuple-element.58), channel_id=1, source_target_pairs={{0,4},{1,5},{2,6},{3,7},{4,8},{5,9},{6,10},{7,11},{8,12},{9,13},{1... | collective-permute-start | bytes 2752520 | tf_op jit(solution)/shard_map/ppermute | solution.py:374
  176.3 47.8 %collective-permute-start.17 = (f32[4,56,8,128]{3,2,1,0:T(8,128)}, f32[4,56,8,128]{3,2,1,0:T(8,128)S(1)}, u32[]{:S(2)}, u32[]{:S(2)}) collective-permute-start(f32[4,56,8,128]{3,2,1,0:T(8,128)} %get-tuple-element.59), channel_id=1, source_target_pairs={{0,8},{1,9},{2,10},{3,11},{4,12},{5,13},{6,14},{7,15},{8,0},{9,1},... | collective-permute-start | bytes 2752520 | tf_op jit(solution)/shard_map/ppermute | solution.py:374
  176.8 50.9 %collective-permute-start.18 = (f32[4,56,8,128]{3,2,1,0:T(8,128)}, f32[4,56,8,128]{3,2,1,0:T(8,128)S(1)}, u32[]{:S(2)}, u32[]{:S(2)}) collective-permute-start(f32[4,56,8,128]{3,2,1,0:T(8,128)} %get-tuple-element.60), channel_id=1, source_target_pairs={{0,12},{1,13},{2,14},{3,15},{4,0},{5,1},{6,2},{7,3},{8,4},{9,5},{1... | collective-permute-start | bytes 2752520 | tf_op jit(solution)/shard_map/ppermute | solution.py:374
  179.1 38.0 %collective-permute-start.4 = (f32[4,57,8,128]{3,2,1,0:T(8,128)}, f32[4,57,8,128]{3,2,1,0:T(8,128)S(1)}, u32[]{:S(2)}, u32[]{:S(2)}) collective-permute-start(f32[4,57,8,128]{3,2,1,0:T(8,128)} %get-tuple-element.43), channel_id=1, source_target_pairs={{0,2},{1,3},{2,0},{3,1},{4,6},{5,7},{6,4},{7,5},{8,10},{9,11},{10,... | collective-permute-start | bytes 2801672 | tf_op jit(solution)/shard_map/ppermute | solution.py:374
  183.9 39.6 %collective-permute-start.5 = (f32[4,57,8,128]{3,2,1,0:T(8,128)}, f32[4,57,8,128]{3,2,1,0:T(8,128)S(1)}, u32[]{:S(2)}, u32[]{:S(2)}) collective-permute-start(f32[4,57,8,128]{3,2,1,0:T(8,128)} %get-tuple-element.44), channel_id=1, source_target_pairs={{0,3},{1,0},{2,1},{3,2},{4,7},{5,4},{6,5},{7,6},{8,11},{9,8},{10,9... | collective-permute-start | bytes 2801672 | tf_op jit(solution)/shard_map/ppermute | solution.py:374
  217.1 11.5 %copy-start.9 = (f32[4,57,8,128]{3,2,1,0:T(8,128)}, f32[4,57,8,128]{3,2,1,0:T(8,128)S(1)}, u32[]{:S(2)}) copy-start(f32[4,57,8,128]{3,2,1,0:T(8,128)S(1)} %collective-permute-done.4.refs_6_) | copy-start | bytes 2801668
  223.4 5.2 %copy-start.10 = (f32[4,57,8,128]{3,2,1,0:T(8,128)}, f32[4,57,8,128]{3,2,1,0:T(8,128)S(1)}, u32[]{:S(2)}) copy-start(f32[4,57,8,128]{3,2,1,0:T(8,128)S(1)} %collective-permute-done.5.refs_7_) | copy-start | bytes 2801668
  224.1 4.5 %copy-start.11 = (f32[4,56,8,128]{3,2,1,0:T(8,128)}, f32[4,56,8,128]{3,2,1,0:T(8,128)S(1)}, u32[]{:S(2)}) copy-start(f32[4,56,8,128]{3,2,1,0:T(8,128)S(1)} %collective-permute-done.16.refs_12_) | copy-start | bytes 2752516
  224.1 3.5 %copy-start.12 = (f32[4,56,8,128]{3,2,1,0:T(8,128)}, f32[4,56,8,128]{3,2,1,0:T(8,128)S(1)}, u32[]{:S(2)}) copy-start(f32[4,56,8,128]{3,2,1,0:T(8,128)S(1)} %collective-permute-done.17.refs_13_) | copy-start | bytes 2752516
  227.6 1.0 copy-start.13
  228.6 36.8 %copy-start.1 = (s32[4,4,2,128]{3,2,1,0:T(2,128)S(1)}, s32[4,4,2,128]{3,2,1,0:T(2,128)}, u32[]{:S(2)}) copy-start(s32[4,4,2,128]{3,2,1,0:T(2,128)} %maximum_convert_fusion) | copy-start | bytes 49156
  228.6 36.8 %copy-start.2 = (f32[32]{0:T(128)S(1)}, f32[32]{0:T(128)}, u32[]{:S(2)}) copy-start(f32[32]{0:T(128)} %reshape.10.refs_0_.refs_1_) | copy-start | bytes 388
  238.4 4.5 %collective-permute-start.19 = (f32[512,128]{1,0:T(8,128)}, f32[512,128]{1,0:T(8,128)S(1)}, u32[]{:S(2)}, u32[]{:S(2)}) collective-permute-start(f32[512,128]{1,0:T(8,128)} %get-tuple-element.62), channel_id=1, source_target_pairs={{0,16},{16,0},{32,48},{48,32},{64,80},{80,64},{96,112},{112,96},{1... | collective-permute-start | bytes 786440 | tf_op jit(solution)/shard_map/ppermute | solution.py:367
  238.4 10.7 %collective-permute-start.20 = (f32[512,128]{1,0:T(8,128)}, f32[512,128]{1,0:T(8,128)S(1)}, u32[]{:S(2)}, u32[]{:S(2)}) collective-permute-start(f32[512,128]{1,0:T(8,128)} %get-tuple-element.63), channel_id=1, source_target_pairs={{0,32},{16,48},{32,64},{48,80},{64,96},{80,112},{96,0},{112,16},{1... | collective-permute-start | bytes 786440 | tf_op jit(solution)/shard_map/ppermute | solution.py:367
  238.6 15.5 %collective-permute-start.21 = (f32[512,128]{1,0:T(8,128)}, f32[512,128]{1,0:T(8,128)S(1)}, u32[]{:S(2)}, u32[]{:S(2)}) collective-permute-start(f32[512,128]{1,0:T(8,128)} %get-tuple-element.64), channel_id=1, source_target_pairs={{0,48},{16,32},{32,80},{48,64},{64,112},{80,96},{96,16},{112,0},{1... | collective-permute-start | bytes 786440 | tf_op jit(solution)/shard_map/ppermute | solution.py:367
  239.5 20.4 %collective-permute-start.22 = (f32[512,128]{1,0:T(8,128)}, f32[512,128]{1,0:T(8,128)S(1)}, u32[]{:S(2)}, u32[]{:S(2)}) collective-permute-start(f32[512,128]{1,0:T(8,128)} %get-tuple-element.65), channel_id=1, source_target_pairs={{0,64},{16,80},{32,96},{48,112},{64,0},{80,16},{96,32},{112,48},{1... | collective-permute-start | bytes 786440 | tf_op jit(solution)/shard_map/ppermute | solution.py:367
  243.0 21.5 %collective-permute-start.23 = (f32[512,128]{1,0:T(8,128)}, f32[512,128]{1,0:T(8,128)S(1)}, u32[]{:S(2)}, u32[]{:S(2)}) collective-permute-start(f32[512,128]{1,0:T(8,128)} %get-tuple-element.66), channel_id=1, source_target_pairs={{0,80},{16,64},{32,112},{48,96},{64,16},{80,0},{96,48},{112,32},{1... | collective-permute-start | bytes 786440 | tf_op jit(solution)/shard_map/ppermute | solution.py:367
  243.0 21.5 %collective-permute-start.24 = (f32[512,128]{1,0:T(8,128)}, f32[512,128]{1,0:T(8,128)S(1)}, u32[]{:S(2)}, u32[]{:S(2)}) collective-permute-start(f32[512,128]{1,0:T(8,128)} %get-tuple-element.67), channel_id=1, source_target_pairs={{0,96},{16,112},{32,0},{48,16},{64,32},{80,48},{96,64},{112,80},{1... | collective-permute-start | bytes 786440 | tf_op jit(solution)/shard_map/ppermute | solution.py:367
  249.1 16.3 %collective-permute-start.25 = (f32[512,128]{1,0:T(8,128)}, f32[512,128]{1,0:T(8,128)S(1)}, u32[]{:S(2)}, u32[]{:S(2)}) collective-permute-start(f32[512,128]{1,0:T(8,128)} %get-tuple-element.68), channel_id=1, source_target_pairs={{0,112},{16,96},{32,16},{48,0},{64,48},{80,32},{96,80},{112,64},{1... | collective-permute-start | bytes 786440 | tf_op jit(solution)/shard_map/ppermute | solution.py:367
  265.4 1.0 copy-start
